TPU v7x, 256 devices: a whole 4x4x8 slice. The times are simulated.
256 devices in a mesh: tm: 8 (over x, core), rows: 32 (over y, z).
Axes of the slice: x: 4, y: 4, z: 8, core: 2. Of those that a mesh axis runs over, the one named last changes fastest.
Arguments:
- latent: bfloat16 [16, 64, 160, 16], P('tm', 'rows'), may hold values from -6 to 6
- entry_kernel: bfloat16 [3, 3, 3, 16, 256], replicated, may hold values from -0.3125 to 0.3125
- middle_kernel: bfloat16 [3, 3, 3, 256, 256], replicated, may hold values from -0.078125 to 0.078125
- upper_kernel: bfloat16 [3, 3, 3, 256, 256], replicated, may hold values from -0.078125 to 0.078125
Outputs:
- decoded: bfloat16 [16, 128, 320, 256], P('tm', 'rows')
All inputs are finite; a program needn't handle non-finite values.
Results may differ from a plain program's by a relative error of at most 0.0059.
Values may be sent and summed in bfloat16 or wider, within the bound.
A program may use at most 64 MiB of HBM per device.

v0:
```python
import jax
import jax.numpy as jnp
from jax import lax
from jax.sharding import PartitionSpec as P


def shifted(block, axis, distance):
    devices = range(lax.axis_size(axis))
    route = [(i - distance, i) for i in devices if i - distance in devices]
    return lax.ppermute(block, axis, route)


def with_halo(array, sides, width):
    for axis, dim in sides:
        size, length = (lax.axis_size(axis), array.shape[dim])
        up = [(i, (i + 1) % size) for i in range(size - 1)]
        down = [(j, i) for i, j in up]
        last = lax.slice_in_dim(array, length - width, length, axis=dim)
        first = lax.slice_in_dim(array, 0, width, axis=dim)
        before = lax.ppermute(last, axis, up)
        after = lax.ppermute(first, axis, down)
        array = jnp.concatenate([before, array, after], axis=dim)
    return array


def convolve(field, weight):
    padded = jnp.pad(field, ((0, 0), (0, 0), (1, 1), (0, 0)))
    result = lax.conv_general_dilated(
        padded[None],
        weight,
        (1, 1, 1),
        "VALID",
        dimension_numbers=("NDHWC", "DHWIO", "NDHWC"),
        preferred_element_type=jnp.float32,
    )
    return result[0]


def per_device(latent, entry_kernel, middle_kernel, upper_kernel):
    frames = latent.shape[0]
    height = latent.shape[1]
    nearer = shifted(latent, "tm", 1)
    farther = shifted(latent, "tm", 2)
    nearer = jnp.concatenate([farther, nearer], 0)
    stretched = jnp.concatenate([nearer, latent], 0)
    rimmed = with_halo(stretched, (("rows", 1),), 2)
    entry = convolve(rimmed, entry_kernel)
    first_row = lax.axis_index("rows") * height - 1
    row_index = first_row + jnp.arange(height + 2, dtype=jnp.int32)
    inside = ((row_index >= 0) & (row_index < height * lax.axis_size("rows"))).astype(jnp.float32)
    widened = (entry * inside[None, :, None, None]).astype(jnp.bfloat16)
    bottom = widened[2:, 1 : height + 1]
    middle = convolve(widened, middle_kernel)
    section_one = (bottom.astype(jnp.float32) + jax.nn.silu(middle)).astype(jnp.bfloat16)
    preceding = shifted(section_one[frames - 2 :], "tm", 1)
    bordered = with_halo(jnp.concatenate([preceding, section_one], 0), (("rows", 1),), 1)
    enlarged = jnp.repeat(jnp.repeat(bordered, 2, axis=1), 2, axis=2)[:, 1:-1]
    return jax.nn.silu(convolve(enlarged, upper_kernel)).astype(jnp.bfloat16)


def solution(mesh):
    return jax.shard_map(
        per_device,
        mesh=mesh,
        in_specs=(P("tm", "rows", None, None), P(), P(), P()),
        out_specs=P("tm", "rows", None, None),
        check_vma=False,
    )
```

profile of v0, /device:TPU:26, one launch (start us, length us, event | category | flops | bytes accessed | tf_op | source)
XLA Modules:
  0.0 101.3 jit_solution(9672255497077271860)
XLA Ops:
  0.0 3.7 %collective-permute-start = (bf16[2,2,160,16]{2,3,1,0:T(8,128)(2,1)}, bf16[2,2,160,16]{2,3,1,0:T(8,128)(2,1)}, u32[]{:S(2)}, u32[]{:S(2)}) collective-permute-start(bf16[2,2,160,16]{2,3,1,0:T(8,128)(2,1)} %param.4), channel_id=1, source_target_pairs={{0,64},{32,96},{64,128},{96,160},{128,192},{160,224},{1,65},{33,97... | collective-permute-start | bytes 61448 | tf_op jit(solution)/shard_map/ppermute | solution.py:10
  3.7 1.9 %collective-permute-start.1 = (bf16[2,2,160,16]{2,3,1,0:T(8,128)(2,1)}, bf16[2,2,160,16]{2,3,1,0:T(8,128)(2,1)}, u32[]{:S(2)}, u32[]{:S(2)}) collective-permute-start(bf16[2,2,160,16]{2,3,1,0:T(8,128)(2,1)} %param.4), channel_id=1, source_target_pairs={{0,32},{32,64},{64,96},{96,128},{128,160},{160,192},{192,224},{1,3... | collective-permute-start | bytes 61448 | tf_op jit(solution)/shard_map/ppermute | solution.py:10
  7.1 2.1 %collective-permute-done.1 = bf16[2,2,160,16]{2,3,1,0:T(8,128)(2,1)} collective-permute-done((bf16[2,2,160,16]{2,3,1,0:T(8,128)(2,1)}, bf16[2,2,160,16]{2,3,1,0:T(8,128)(2,1)}, u32[]{:S(2)}, u32[]{:S(2)}) %collective-permute-start.1) | collective-permute-done | bytes 20512 | tf_op jit(solution)/shard_map/ppermute | solution.py:10
  10.7 7.9 %collective-permute-start.3 = (bf16[6,2,160,16]{2,3,1,0:T(8,128)(2,1)S(1)}, bf16[6,2,160,16]{2,3,1,0:T(8,128)(2,1)S(1)}, u32[]{:S(2)}, u32[]{:S(2)}) collective-permute-start(bf16[6,2,160,16]{2,3,1,0:T(8,128)(2,1)S(1)} %constant_dynamic-update-slice_fusion), channel_id=1, source_target_pairs={{1,0},{2,1},{3,2},{4,3},{5,4},{6,5},{7,6},{8,7},{9,8},{10,9},{11,1... | collective-permute-start | bytes 184328 | tf_op jit(solution)/shard_map/ppermute | solution.py:21
  18.7 1.9 %collective-permute-start.2 = (bf16[6,2,160,16]{2,3,1,0:T(8,128)(2,1)S(1)}, bf16[6,2,160,16]{2,3,1,0:T(8,128)(2,1)S(1)}, u32[]{:S(2)}, u32[]{:S(2)}) collective-permute-start(bf16[6,2,160,16]{2,3,1,0:T(8,128)(2,1)S(1)} %constant_dynamic-update-slice_fusion), channel_id=1, source_target_pairs={{0,1},{1,2},{2,3},{3,4},{4,5},{5,6},{6,7},{7,8},{8,9},{9,10},{10,1... | collective-permute-start | bytes 184328 | tf_op jit(solution)/shard_map/ppermute | solution.py:20
  20.9 6.4 %collective-permute-done.2 = bf16[6,2,160,16]{2,3,1,0:T(8,128)(2,1)S(1)} collective-permute-done((bf16[6,2,160,16]{2,3,1,0:T(8,128)(2,1)S(1)}, bf16[6,2,160,16]{2,3,1,0:T(8,128)(2,1)S(1)}, u32[]{:S(2)}, u32[]{:S(2)}) %collective-permute-start.2) | collective-permute-done | bytes 61472 | tf_op jit(solution)/shard_map/ppermute | solution.py:20
  28.2 2.6 %reshape.18 = bf16[6,6,1,8,21,16]{4,3,5,1,0,2:T(8,128)(2,1)} reshape(bf16[6,6,1,168,16]{3,4,1,0,2:T(8,128)(2,1)} %pad.15) | data formatting | bytes 387072 | tf_op jit(solution)/shard_map/conv_general_dilated | solution.py:28
  30.9 4.1 %copy.32 = bf16[6,6,1,8,21,16]{5,3,4,1,0,2:T(8,128)(2,1)} copy(bf16[6,6,1,8,21,16]{4,3,5,1,0,2:T(8,128)(2,1)} %reshape.18) | data formatting | bytes 387072 | tf_op jit(solution)/shard_map/conv_general_dilated | solution.py:28
  35.9 3.6 %fusion.20 = f32[4,4,8,21,256]{4,2,3,1,0:T(8,128)S(1)} fusion(bf16[3,3,3,16,256]{4,3,2,1,0:T(8,128)(2,1)} %param.5, bf16[6,6,1,7,2,16]{5,3,4,1,0,2:T(8,128)(2,1)S(1)} %slice.22, bf16[6,6,1,8,21,16]{5,3,4,1,0,2:T(8,128)(2,1)} %copy.32, pred[8,21]{0,1:T(8,128)(4,1)S(1)} %copy-done.3), kind=kOutput, calls=%fused_computation.25 | convolution fusion | flops 595866624 | bytes 3183528 | tf_op jit(solution)/shard_map/conv_general_dilated | solution.py:28
  43.7 2.6 %fusion.33 = f32[2,2,8,21,256]{4,2,3,1,0:T(8,128)S(1)} fusion(bf16[3,3,3,256,256]{4,3,2,1,0:T(8,128)(2,1)S(1)} %copy-done.1, bf16[4,4,1,7,2,256]{5,3,4,1,0,2:T(8,128)(2,1)S(1)} %slice.25, bf16[4,4,1,8,21,256]{5,3,4,1,0,2:T(8,128)(2,1)S(1)} %copy.35, pred[8,21]{0,1:T(8,128)(4,1)S(1)} %copy-done.3), kind=kOutput, calls=%fused_computation.35 | convolution fusion | flops 2382864384 | bytes 5718184 | tf_op jit(solution)/shard_map/conv_general_dilated | solution.py:28
  47.6 1.9 %collective-permute-start.4 = (bf16[2,2,160,256]{3,1,2,0:T(2,128)(2,1)S(1)}, bf16[2,2,160,256]{3,1,2,0:T(2,128)(2,1)S(1)}, u32[]{:S(2)}, u32[]{:S(2)}) collective-permute-start(bf16[2,2,160,256]{3,1,2,0:T(2,128)(2,1)S(1)} %fusion.39), channel_id=1, source_target_pairs={{0,32},{32,64},{64,96},{96,128},{128,160},{160,192},{192,224},{1,3... | collective-permute-start | bytes 983048 | tf_op jit(solution)/shard_map/ppermute | solution.py:10
  49.5 6.5 %collective-permute-done.4 = bf16[2,2,160,256]{3,1,2,0:T(2,128)(2,1)S(1)} collective-permute-done((bf16[2,2,160,256]{3,1,2,0:T(2,128)(2,1)S(1)}, bf16[2,2,160,256]{3,1,2,0:T(2,128)(2,1)S(1)}, u32[]{:S(2)}, u32[]{:S(2)}) %collective-permute-start.4) | collective-permute-done | bytes 327712 | tf_op jit(solution)/shard_map/ppermute | solution.py:10
  57.1 2.1 %collective-permute-start.6 = (bf16[4,1,160,256]{3,2,1,0:T(8,128)(2,1)S(1)}, bf16[4,1,160,256]{3,2,1,0:T(8,128)(2,1)S(1)}, u32[]{:S(2)}, u32[]{:S(2)}) collective-permute-start(bf16[4,1,160,256]{3,2,1,0:T(8,128)(2,1)S(1)} %copy.38), channel_id=1, source_target_pairs={{1,0},{2,1},{3,2},{4,3},{5,4},{6,5},{7,6},{8,7},{9,8},{10,9},{11,1... | collective-permute-start | bytes 983048 | tf_op jit(solution)/shard_map/ppermute | solution.py:21
  59.3 3.9 %collective-permute-start.5 = (bf16[4,1,160,256]{3,2,1,0:T(8,128)(2,1)S(1)}, bf16[4,1,160,256]{3,2,1,0:T(8,128)(2,1)S(1)}, u32[]{:S(2)}, u32[]{:S(2)}) collective-permute-start(bf16[4,1,160,256]{3,2,1,0:T(8,128)(2,1)S(1)} %copy.37), channel_id=1, source_target_pairs={{0,1},{1,2},{2,3},{3,4},{4,5},{5,6},{6,7},{7,8},{8,9},{9,10},{10,1... | collective-permute-start | bytes 983048 | tf_op jit(solution)/shard_map/ppermute | solution.py:20
  63.2 4.2 %collective-permute-done.6 = bf16[4,1,160,256]{3,2,1,0:T(8,128)(2,1)S(1)} collective-permute-done((bf16[4,1,160,256]{3,2,1,0:T(8,128)(2,1)S(1)}, bf16[4,1,160,256]{3,2,1,0:T(8,128)(2,1)S(1)}, u32[]{:S(2)}, u32[]{:S(2)}) %collective-permute-start.6) | collective-permute-done | bytes 327712 | tf_op jit(solution)/shard_map/ppermute | solution.py:21
  68.0 3.8 %collective-permute-done.5 = bf16[4,1,160,256]{3,2,1,0:T(8,128)(2,1)S(1)} collective-permute-done((bf16[4,1,160,256]{3,2,1,0:T(8,128)(2,1)S(1)}, bf16[4,1,160,256]{3,2,1,0:T(8,128)(2,1)S(1)}, u32[]{:S(2)}, u32[]{:S(2)}) %collective-permute-start.5) | collective-permute-done | bytes 327712 | tf_op jit(solution)/shard_map/ppermute | solution.py:20
  72.3 2.3 %pad_maximum_fusion = bf16[4,4,160,256]{3,1,2,0:T(4,128)(2,1)S(1)} fusion(bf16[4,1,160,256]{3,1,2,0:T(2,128)(2,1)S(1)} %copy.40, bf16[2,2,160,256]{3,1,2,0:T(2,128)(2,1)S(1)} %fusion.39, bf16[2,2,160,256]{3,1,2,0:T(2,128)(2,1)S(1)} %collective-permute-done.4, bf16[4,1,160,256]{3,1,2,0:T(2,128)(2,1)S(1)} %copy.39), kind=kLoop, calls=%fused_computation.34 | loop fusion | flops 5242880 | bytes 2621440 | tf_op jit(solution)/shard_map/concatenate | solution.py:22
  75.6 2.2 %broadcast_in_dim.18 = bf16[4,4,2,160,256]{4,0,3,2,1:T(4,128)(2,1)} broadcast(bf16[4,4,160,256]{3,0,2,1:T(4,128)(2,1)S(1)} %copy.41), dimensions={0,1,3,4} | broadcast | bytes 3932160 | tf_op jit(solution)/shard_map/broadcast_in_dim | solution.py:57
  77.8 3.1 %broadcast_in_dim.19 = bf16[4,8,160,2,256]{4,0,3,2,1:T(4,128)(2,1)S(1)} broadcast(bf16[4,8,160,256]{3,0,2,1:T(4,128)(2,1)} %bitcast.55), dimensions={0,1,2,4} | broadcast | bytes 7864320 | tf_op jit(solution)/shard_map/broadcast_in_dim | solution.py:57
  80.9 1.4 %slice.29 = bf16[4,6,320,256]{3,0,2,1:T(4,128)(2,1)S(1)} slice(bf16[4,8,320,256]{3,0,2,1:T(4,128)(2,1)S(1)} %bitcast.52), slice={[0:4], [1:7], [0:320], [0:256]} | slice | bytes 7864320 | tf_op jit(solution)/shard_map/slice | solution.py:57
  82.3 1.7 %pad_bitcast_fusion = bf16[4,6,1,322,256]{4,0,3,1,2:T(4,128)(2,1)S(1)} fusion(bf16[4,6,320,256]{3,0,2,1:T(4,128)(2,1)S(1)} %slice.29), kind=kLoop, calls=%fused_computation.8 | loop fusion | bytes 7888896 | tf_op jit(solution)/shard_map/broadcast_in_dim | solution.py:29
  84.0 1.5 %pad.19 = bf16[4,6,1,328,256]{4,0,3,1,2:T(4,128)(2,1)S(1)} pad(bf16[4,6,1,322,256]{4,0,3,1,2:T(4,128)(2,1)S(1)} %pad_bitcast_fusion, bf16[]{:T(256)} %constant.7.clone.1), padding=0_0x0_0x0_0x0_6x0_0 | pad | bytes 7987202 | tf_op jit(solution)/shard_map/broadcast_in_dim | solution.py:29
  86.2 11.7 %fusion.23 = f32[2,4,8,41,256]{4,2,3,1,0:T(8,128)S(1)} fusion(bf16[3,3,3,256,256]{4,3,2,1,0:T(8,128)(2,1)S(1)} %copy-done, bf16[4,6,1,7,2,256]{5,3,4,1,0,2:T(8,128)(2,1)S(1)} %slice.30, bf16[4,6,1,8,41,256]{5,3,4,1,0,2:T(8,128)(2,1)S(1)} %copy.43, pred[8,41]{0,1:T(8,128)(4,1)S(1)} %copy-done.2), kind=kOutput, calls=%fused_computation.26 | convolution fusion | flops 9299542016 | bytes 10428744 | tf_op jit(solution)/shard_map/conv_general_dilated | solution.py:28
  99.5 1.8 %multiply_convert_fusion = bf16[2,4,320,256]{3,2,1,0:T(8,128)(2,1)} fusion(f32[2,4,1,320,256]{4,1,3,0,2:T(4,128)S(1)} %slice.31), kind=kLoop, calls=%fused_computation.17 | loop fusion | flops 3276800 | bytes 3932160 | tf_op jit(solution)/shard_map/convert_element_type | solution.py:58
  (35 shorter events, 16.0 us)
Async XLA Ops:
  0.0 86.1 %copy-start = (bf16[3,3,3,256,256]{4,3,2,1,0:T(8,128)(2,1)S(1)}, bf16[3,3,3,256,256]{4,3,2,1,0:T(8,128)(2,1)}, u32[]{:S(2)}) copy-start(bf16[3,3,3,256,256]{4,3,2,1,0:T(8,128)(2,1)} %param.7) | copy-start | bytes 10616836
  0.0 6.4 %collective-permute-start = (bf16[2,2,160,16]{2,3,1,0:T(8,128)(2,1)}, bf16[2,2,160,16]{2,3,1,0:T(8,128)(2,1)}, u32[]{:S(2)}, u32[]{:S(2)}) collective-permute-start(bf16[2,2,160,16]{2,3,1,0:T(8,128)(2,1)} %param.4), channel_id=1, source_target_pairs={{0,64},{32,96},{64,128},{96,160},{128,192},{160,224},{1,65},{33,97... | collective-permute-start | bytes 61448 | tf_op jit(solution)/shard_map/ppermute | solution.py:10
  3.7 5.6 %collective-permute-start.1 = (bf16[2,2,160,16]{2,3,1,0:T(8,128)(2,1)}, bf16[2,2,160,16]{2,3,1,0:T(8,128)(2,1)}, u32[]{:S(2)}, u32[]{:S(2)}) collective-permute-start(bf16[2,2,160,16]{2,3,1,0:T(8,128)(2,1)} %param.4), channel_id=1, source_target_pairs={{0,32},{32,64},{64,96},{96,128},{128,160},{160,192},{192,224},{1,3... | collective-permute-start | bytes 61448 | tf_op jit(solution)/shard_map/ppermute | solution.py:10
  10.7 10.1 %collective-permute-start.3 = (bf16[6,2,160,16]{2,3,1,0:T(8,128)(2,1)S(1)}, bf16[6,2,160,16]{2,3,1,0:T(8,128)(2,1)S(1)}, u32[]{:S(2)}, u32[]{:S(2)}) collective-permute-start(bf16[6,2,160,16]{2,3,1,0:T(8,128)(2,1)S(1)} %constant_dynamic-update-slice_fusion), channel_id=1, source_target_pairs={{1,0},{2,1},{3,2},{4,3},{5,4},{6,5},{7,6},{8,7},{9,8},{10,9},{11,1... | collective-permute-start | bytes 184328 | tf_op jit(solution)/shard_map/ppermute | solution.py:21
  18.7 8.6 %collective-permute-start.2 = (bf16[6,2,160,16]{2,3,1,0:T(8,128)(2,1)S(1)}, bf16[6,2,160,16]{2,3,1,0:T(8,128)(2,1)S(1)}, u32[]{:S(2)}, u32[]{:S(2)}) collective-permute-start(bf16[6,2,160,16]{2,3,1,0:T(8,128)(2,1)S(1)} %constant_dynamic-update-slice_fusion), channel_id=1, source_target_pairs={{0,1},{1,2},{2,3},{3,4},{4,5},{5,6},{6,7},{7,8},{8,9},{9,10},{10,1... | collective-permute-start | bytes 184328 | tf_op jit(solution)/shard_map/ppermute | solution.py:20
  27.5 8.4 %copy-start.3 = (pred[8,21]{0,1:T(8,128)(4,1)S(1)}, pred[8,21]{0,1:T(8,128)(4,1)}, u32[]{:S(2)}) copy-start(pred[8,21]{0,1:T(8,128)(4,1)} %constant.41) | copy-start | bytes 508
  41.7 2.0 %copy-start.1 = (bf16[3,3,3,256,256]{4,3,2,1,0:T(8,128)(2,1)S(1)}, bf16[3,3,3,256,256]{4,3,2,1,0:T(8,128)(2,1)}, u32[]{:S(2)}) copy-start(bf16[3,3,3,256,256]{4,3,2,1,0:T(8,128)(2,1)} %param.6) | copy-start | bytes 10616836
  47.6 8.4 %collective-permute-start.4 = (bf16[2,2,160,256]{3,1,2,0:T(2,128)(2,1)S(1)}, bf16[2,2,160,256]{3,1,2,0:T(2,128)(2,1)S(1)}, u32[]{:S(2)}, u32[]{:S(2)}) collective-permute-start(bf16[2,2,160,256]{3,1,2,0:T(2,128)(2,1)S(1)} %fusion.39), channel_id=1, source_target_pairs={{0,32},{32,64},{64,96},{96,128},{128,160},{160,192},{192,224},{1,3... | collective-permute-start | bytes 983048 | tf_op jit(solution)/shard_map/ppermute | solution.py:10
  57.1 10.3 %collective-permute-start.6 = (bf16[4,1,160,256]{3,2,1,0:T(8,128)(2,1)S(1)}, bf16[4,1,160,256]{3,2,1,0:T(8,128)(2,1)S(1)}, u32[]{:S(2)}, u32[]{:S(2)}) collective-permute-start(bf16[4,1,160,256]{3,2,1,0:T(8,128)(2,1)S(1)} %copy.38), channel_id=1, source_target_pairs={{1,0},{2,1},{3,2},{4,3},{5,4},{6,5},{7,6},{8,7},{9,8},{10,9},{11,1... | collective-permute-start | bytes 983048 | tf_op jit(solution)/shard_map/ppermute | solution.py:21
  59.3 12.4 %collective-permute-start.5 = (bf16[4,1,160,256]{3,2,1,0:T(8,128)(2,1)S(1)}, bf16[4,1,160,256]{3,2,1,0:T(8,128)(2,1)S(1)}, u32[]{:S(2)}, u32[]{:S(2)}) collective-permute-start(bf16[4,1,160,256]{3,2,1,0:T(8,128)(2,1)S(1)} %copy.37), channel_id=1, source_target_pairs={{0,1},{1,2},{2,3},{3,4},{4,5},{5,6},{6,7},{7,8},{8,9},{9,10},{10,1... | collective-permute-start | bytes 983048 | tf_op jit(solution)/shard_map/ppermute | solution.py:20
  85.5 0.7 copy-start.2
where the time goes:
time: 102 us; the launch traced here: 101 us
  local copies, waits for them, and re-layouts  28.8 us (28%)
  waiting for transfers between devices  24 us (24%)
  starting transfers between devices  23.4 us (23%)
  matrix products  18 us (18%)
  other arithmetic  6.8 us (7%)
    conv_general_dilated x3, matrix products, convolve(): lax.conv_general_dilated(padded[None], weight, (1, 1, 1), 'VALID', dimens...  18 us
    conv_general_dilated x11, local copies, waits for them, and re-layouts, convolve(): lax.conv_general_dilated(padded[None], weight, (1, 1, 1), 'VALID', dimens...  11.3 us
    ppermute x2, waiting for transfers between devices, with_halo(): before = lax.ppermute(last, axis, up)  10.2 us
    ppermute x2, starting transfers between devices, with_halo(): after = lax.ppermute(first, axis, down)  10 us
    ppermute x3, waiting for transfers between devices, shifted(): return lax.ppermute(block, axis, route)  9.32 us
    ppermute x3, starting transfers between devices, shifted(): return lax.ppermute(block, axis, route)  7.5 us
    ppermute x2, starting transfers between devices, with_halo(): before = lax.ppermute(last, axis, up)  5.84 us
    broadcast_in_dim x2, local copies, waits for them, and re-layouts, per_device(): enlarged = jnp.repeat(jnp.repeat(bordered, 2, axis=1), 2, axis=2)[:, 1:-1]  5.29 us
  transfers between devices with their start and end apart: 7, of which 7 were waited for; matrix products, arithmetic and copies ran while one was open for 1% of the time, Pallas kernels for 0%

commit v1 on v0

v1 whole, which is shorter than its diff:
```python
import jax
import jax.numpy as jnp
from jax import lax
from jax.experimental import pallas as pl
from jax.experimental.pallas import tpu as pltpu
from jax.sharding import PartitionSpec as P

F32 = jnp.float32
BF = jnp.bfloat16
W = 160
C = 256
CI = 16
NBACK = 3
NSIDE = 2


def roll_cols(x, d):
    n = x.shape[0]
    row = lax.broadcasted_iota(jnp.int32, x.shape, 0)
    if d == 0:
        return jnp.where(row == 0, 0.0, pltpu.roll(x, 1, 0))
    return jnp.where(row == n - 1, 0.0, pltpu.roll(x, n - 1, 0))


def silu(v):
    return v * (1.0 / (1.0 + jnp.exp(-v)))


def put3(dst, idx, x):
    for d in range(3):
        y = x if d == 1 else roll_cols(x, d)
        dst[(d,) + idx] = y.astype(BF)


def partners():
    return [(i, j) for i in range(NBACK + 1) for j in range(-NSIDE, NSIDE + 1) if (i, j) != (0, 0)]


def exchange_body(nt, nr, lat, ek, uk, R, WE, WU, ubuf, usem, ssem, rsem):
    me_t = lax.axis_index("tm")
    me_r = lax.axis_index("rows")

    def there(di, dj):
        t = me_t + di
        r = me_r + dj
        return (t >= 0) & (t < nt) & (r >= 0) & (r < nr)

    def to(di, dj):
        return {"tm": me_t + di, "rows": me_r + dj}

    load = pltpu.make_async_copy(uk, ubuf, usem)
    load.start()
    barrier = pltpu.get_barrier_semaphore()
    for i, j in partners():
        @pl.when(there(-i, -j))
        def _():
            pl.semaphore_signal(barrier, inc=1, device_id=to(-i, -j), device_id_type=pl.DeviceIdType.MESH)
    R[6:8, 3:5] = lat[...]
    slots = {-2: (7, 8), -1: (5, 7), 0: (3, 5), 1: (1, 3), 2: (0, 1)}
    for i, j in partners():
        lo, hi = slots[j]

        @pl.when(jnp.logical_not(there(-i, -j)))
        def _():
            R[6 - 2 * i:8 - 2 * i, lo:hi] = jnp.zeros((2, hi - lo, CI, W), BF)
    ahead = jnp.minimum(nt - 1 - me_t, NBACK) + 1
    beside = jnp.minimum(me_r, NSIDE) + jnp.minimum(nr - 1 - me_r, NSIDE) + 1
    pl.semaphore_wait(barrier, ahead * beside - 1)

    def copy(n, i, j):
        lo, hi = slots[j]
        if j == 2:
            src = lat.at[:, 1:2]
        elif j == -2:
            src = lat.at[:, 0:1]
        else:
            src = lat
        return pltpu.make_async_remote_copy(
            src_ref=src,
            dst_ref=R.at[6 - 2 * i:8 - 2 * i, lo:hi],
            send_sem=ssem.at[n],
            recv_sem=rsem.at[n],
            device_id=to(i, j),
            device_id_type=pl.DeviceIdType.MESH,
        )

    for n, (i, j) in enumerate(partners()):
        @pl.when(there(i, j))
        def _():
            copy(n, i, j).start()

    WE[...] = jnp.zeros(WE.shape, BF)
    for dc in range(3):
        for dt in range(3):
            for dr in range(3):
                w = ek[dt, dr, dc]
                for fo in range(2):
                    for ro in range(2):
                        k = ((fo + dt) * 4 + ro + dr) * CI
                        n = (fo * 2 + ro) * C
                        WE[dc, k:k + CI, n:n + C] = w
    load.wait()

    def fold(s, carry):
        dt = s // 8
        r0 = pl.multiple_of((s % 8) * 32, 32)
        m = [[ubuf[dt, r, c, pl.ds(r0, 32), :].astype(F32) for c in range(3)] for r in range(3)]
        rows = [[m[0], [m[1][c] + m[2][c] for c in range(3)]],
                [[m[0][c] + m[1][c] for c in range(3)], m[2]]]
        for a in range(2):
            for e in range(2):
                q = rows[a][e]
                cols = [[q[0], q[1] + q[2]], [q[0] + q[1], q[2]]]
                for b in range(2):
                    for c in range(2):
                        WU[a, b, dt, e, c, pl.ds(r0, 32), :] = cols[b][c].astype(BF)
        return carry

    lax.fori_loop(0, 24, fold, 0)

    for n, (i, j) in enumerate(partners()):
        @pl.when(there(i, j))
        def _():
            copy(n, i, j).wait_send()

        @pl.when(there(-i, -j))
        def _():
            copy(n, i, j).wait_recv()


def exchange(nt, nr, lat, ek, uk):
    vm = pl.BlockSpec(memory_space=pltpu.VMEM)
    n = len(partners())

    def body(*refs):
        exchange_body(nt, nr, *refs)

    return pl.pallas_call(
        body,
        out_shape=(
            jax.ShapeDtypeStruct((8, 8, CI, W), BF),
            jax.ShapeDtypeStruct((3, 256, 1024), BF),
            jax.ShapeDtypeStruct((2, 2, 3, 2, 2, C, C), BF),
        ),
        in_specs=[vm, vm, pl.BlockSpec(memory_space=pl.ANY)],
        out_specs=(vm, vm, vm),
        scratch_shapes=[
            pltpu.VMEM((3, 3, 3, C, C), BF),
            pltpu.SemaphoreType.DMA,
            pltpu.SemaphoreType.DMA((n,)),
            pltpu.SemaphoreType.DMA((n,)),
        ],
        compiler_params=pltpu.CompilerParams(collective_id=0, has_side_effects=True, vmem_limit_bytes=16 * 2**20),
        name="exchange",
    )(lat, ek, uk)


def decode_body(n_rows, height, R, WE, W2, WU, out, V, B3, S3, I):
    row_base = lax.axis_index("rows") * height
    for g in range(3):
        for fp in range(4):
            y = R[2 * fp:2 * fp + 2, 2 * g:2 * g + 4].reshape(128, W).astype(F32).T
            for d in range(3):
                z = y if d == 1 else roll_cols(y, d)
                V[d, g, fp] = z.astype(BF)
    for g in range(3):
        for fo in range(2):
            acc = None
            for d in range(3):
                lhs = jnp.concatenate(
                    [jnp.concatenate([V[d, g, k], V[d, g, k + 1]], axis=1) for k in range(3)], axis=0)
                p = jnp.dot(lhs, WE[d, :, fo * 512:(fo + 1) * 512], preferred_element_type=F32)
                acc = p if acc is None else acc + p
            for ro in range(2):
                gr = row_base - 2 + 2 * g + ro
                ok = jnp.where((gr >= 0) & (gr < n_rows), 1.0, 0.0)
                for k in range(3):
                    put3(B3, (2 * k + fo, 2 * g + ro), acc[k * W:(k + 1) * W, ro * C:(ro + 1) * C] * ok)

    def mid(f, carry):
        acc = None
        for dt in range(3):
            for dr in range(3):
                for dc in range(3):
                    lhs = B3[dc, f + dt, dr:dr + 4].reshape(4 * W, C)
                    p = jnp.dot(lhs, W2[dt, dr, dc], preferred_element_type=F32)
                    acc = p if acc is None else acc + p
        for r in range(4):
            gr = row_base - 1 + r
            ok = jnp.where((gr >= 0) & (gr < n_rows), 1.0, 0.0)
            s = (B3[1, f + 2, r + 1].astype(F32) + silu(acc[r * W:(r + 1) * W])) * ok
            put3(S3, (f, r), s)
        return carry

    lax.fori_loop(0, 4, mid, 0)
    for a in range(2):
        for b in range(2):
            acc = None
            for dt in range(3):
                for e in range(2):
                    for c in range(2):
                        lhs = jnp.concatenate(
                            [S3[b + c, t + dt, a + e + q] for t in range(2) for q in range(2)], axis=0)
                        p = jnp.dot(lhs, WU[a, b, dt, e, c], preferred_element_type=F32)
                        acc = p if acc is None else acc + p
            y = silu(acc)
            for i in range(4):
                for h in range(2):
                    I[i, h, pl.ds(b, W, stride=2), :] = y[i * W:(i + 1) * W, h * 128:(h + 1) * 128]
        for i in range(4):
            for h in range(2):
                out[i // 2, 2 * (i % 2) + a, :, h * 128:(h + 1) * 128] = I[i, h].astype(BF)


def decode(n_rows, height, R, WE, W2, WU):
    vm = pl.BlockSpec(memory_space=pltpu.VMEM)

    def body(*refs):
        decode_body(n_rows, height, *refs)

    return pl.pallas_call(
        body,
        out_shape=jax.ShapeDtypeStruct((2, 4, 2 * W, C), BF),
        in_specs=[vm, vm, vm, vm],
        out_specs=vm,
        scratch_shapes=[
            pltpu.VMEM((3, 3, 4, W, 128), BF),
            pltpu.VMEM((3, 6, 6, W, C), BF),
            pltpu.VMEM((3, 4, 4, W, C), BF),
            pltpu.VMEM((4, 2, 2 * W, 128), F32),
        ],
        compiler_params=pltpu.CompilerParams(vmem_limit_bytes=40 * 2**20),
        name="decode",
    )(R, WE, W2, WU)


def per_device(nt, nr, latent, entry_kernel, middle_kernel, upper_kernel):
    height = latent.shape[1]
    lat = jnp.transpose(latent, (0, 1, 3, 2))
    R, WE, WU = exchange(nt, nr, lat, entry_kernel, pltpu.with_memory_space_constraint(upper_kernel, pltpu.HBM))
    return decode(height * nr, height, R, WE, middle_kernel, WU)


def solution(mesh):
    nt = mesh.shape["tm"]
    nr = mesh.shape["rows"]
    return jax.shard_map(
        lambda *a: per_device(nt, nr, *a),
        mesh=mesh,
        in_specs=(P("tm", "rows", None, None), P(), P(), P()),
        out_specs=P("tm", "rows", None, None),
        check_vma=False,
    )
```

time: 102 us -> 38.8 us (0.38)
  the two profiles are of different devices: /device:TPU:26 before, /device:TPU:28 now
where the time goes in v1:
time: 38.8 us; the launch traced here: 38.7 us
  Pallas kernels  36.8 us (95%)
  local copies, waits for them, and re-layouts  1.93 us (5%)
    pallas_call x1, Pallas kernels, decode(): pl.pallas_call(body, out_shape=jax.ShapeDtypeStruct((2, 4, 2 * W, C), BF)...  19.5 us
    pallas_call x1, Pallas kernels, exchange(): pl.pallas_call(body, out_shape=(jax.ShapeDtypeStruct((8, 8, CI, W), BF),...  17.3 us
    unnamed x6, local copies, waits for them, and re-layouts  1.93 us

profile of v1, /device:TPU:28, one launch (start us, length us, event | category | flops | bytes accessed | tf_op | source)
XLA Modules:
  0.0 38.7 jit_solution(2235135215229709265)
XLA Ops:
  0.0 0.0 copy-start
  0.0 0.0 copy-start.1
  0.0 1.1 %copy-done.1 = bf16[3,3,3,16,256]{4,3,2,1,0:T(8,128)(2,1)S(1)} copy-done((bf16[3,3,3,16,256]{4,3,2,1,0:T(8,128)(2,1)S(1)}, bf16[3,3,3,16,256]{4,3,2,1,0:T(8,128)(2,1)}, u32[]{:S(2)}) %copy-start.1) | copy-done | bytes 221208
  1.1 0.0 copy-start.2
  1.1 0.8 %copy-done.2 = bf16[2,2,160,16]{2,3,1,0:T(8,128)(2,1)S(1)} copy-done((bf16[2,2,160,16]{2,3,1,0:T(8,128)(2,1)S(1)}, bf16[2,2,160,16]{2,3,1,0:T(8,128)(2,1)}, u32[]{:S(2)}) %copy-start.2) | copy-done | bytes 20504
  1.9 17.3 %exchange.1 = (bf16[8,8,16,160]{3,2,1,0:T(8,128)(2,1)S(1)}, bf16[3,256,1024]{2,1,0:T(8,128)(2,1)S(1)}, bf16[2,2,3,2,2,256,256]{6,5,4,3,2,1,0:T(8,128)(2,1)S(1)}) custom-call(bf16[2,2,16,160]{3,2,1,0:T(8,128)(2,1)S(1)} %bitcast.1, bf16[3,3,3,16,256]{4,3,2,1,0:T(8,128)(2,1)S(1)} %copy-done.1, bf16[3,3,3,256,256]{4,3,2,1,0:T(8,128)(2,1)} %refs_2_.2), custom_call_target="tpu_custom_call" | custom-call | tf_op jit(solution)/shard_map/exchange/pallas_call | solution.py:138
  19.2 0.0 copy-done
  19.2 19.5 %decode.1 = bf16[2,4,320,256]{3,2,1,0:T(8,128)(2,1)} custom-call(bf16[8,8,16,160]{3,2,1,0:T(8,128)(2,1)S(1)} %get-tuple-element.8.refs_0_, bf16[3,256,1024]{2,1,0:T(8,128)(2,1)S(1)} %get-tuple-element.9.refs_1_, bf16[3,3,3,256,256]{4,3,2,1,0:T(8,128)(2,1)S(1)} %copy-done, bf16[2,2,3,2,2,256,256]{6,5,4,3,2,1,0:T(8,128)(2,1)S(1)} %get-tuple-element.10.refs_3_), custom_call_target="tpu_custom_call" | custom-call | tf_op jit(solution)/shard_map/decode/pallas_call | solution.py:221
Async XLA Ops:
  0.0 19.2 %copy-start = (bf16[3,3,3,256,256]{4,3,2,1,0:T(8,128)(2,1)S(1)}, bf16[3,3,3,256,256]{4,3,2,1,0:T(8,128)(2,1)}, u32[]{:S(2)}) copy-start(bf16[3,3,3,256,256]{4,3,2,1,0:T(8,128)(2,1)} %refs_2_.3) | copy-start | bytes 10616836
  0.0 1.1 %copy-start.1 = (bf16[3,3,3,16,256]{4,3,2,1,0:T(8,128)(2,1)S(1)}, bf16[3,3,3,16,256]{4,3,2,1,0:T(8,128)(2,1)}, u32[]{:S(2)}) copy-start(bf16[3,3,3,16,256]{4,3,2,1,0:T(8,128)(2,1)} %refs_1_.1) | copy-start | bytes 663556
  1.1 0.8 %copy-start.2 = (bf16[2,2,160,16]{2,3,1,0:T(8,128)(2,1)S(1)}, bf16[2,2,160,16]{2,3,1,0:T(8,128)(2,1)}, u32[]{:S(2)}) copy-start(bf16[2,2,160,16]{2,3,1,0:T(8,128)(2,1)} %param.4) | copy-start | bytes 61444

commit v2 on v1

--- a/solution.py
+++ b/solution.py
@@ -36,7 +36,10 @@
     return [(i, j) for i in range(NBACK + 1) for j in range(-NSIDE, NSIDE + 1) if (i, j) != (0, 0)]
 
 
-def exchange_body(nt, nr, lat, ek, uk, R, WE, WU, ubuf, usem, ssem, rsem):
+ROW_OF = ((0, 1), (1, 0), (1, 1), (2, 0), (2, 1), (3, 0), (3, 1), (4, 0))
+
+
+def exchange_body(nt, nr, lat_h, ek_h, uk, R, WE, WU, lat, ek, ubuf, pack, lsem, ssem, rsem):
     me_t = lax.axis_index("tm")
     me_r = lax.axis_index("rows")
 
@@ -48,36 +51,37 @@
     def to(di, dj):
         return {"tm": me_t + di, "rows": me_r + dj}
 
-    load = pltpu.make_async_copy(uk, ubuf, usem)
-    load.start()
+    loads = [pltpu.make_async_copy(src, dst, lsem.at[n])
+             for n, (src, dst) in enumerate(((lat_h, lat), (ek_h, ek), (uk, ubuf)))]
+    for x in loads:
+        x.start()
     barrier = pltpu.get_barrier_semaphore()
     for i, j in partners():
         @pl.when(there(-i, -j))
         def _():
             pl.semaphore_signal(barrier, inc=1, device_id=to(-i, -j), device_id_type=pl.DeviceIdType.MESH)
-    R[6:8, 3:5] = lat[...]
-    slots = {-2: (7, 8), -1: (5, 7), 0: (3, 5), 1: (1, 3), 2: (0, 1)}
     for i, j in partners():
-        lo, hi = slots[j]
-
         @pl.when(jnp.logical_not(there(-i, -j)))
         def _():
-            R[6 - 2 * i:8 - 2 * i, lo:hi] = jnp.zeros((2, hi - lo, CI, W), BF)
+            R[NBACK - i, 2 - j] = jnp.zeros((5, CI, 128), BF)
+    loads[0].wait()
+    tails = []
+    for r in range(2):
+        for f in range(2):
+            v = lat[f, r]
+            pack[3 * r + f] = v[:, :128]
+            tails.append(v[:, 128:].astype(F32))
+    pack[2] = jnp.concatenate(tails, axis=1).astype(BF)
+    R[NBACK, 2] = pack[...]
     ahead = jnp.minimum(nt - 1 - me_t, NBACK) + 1
     beside = jnp.minimum(me_r, NSIDE) + jnp.minimum(nr - 1 - me_r, NSIDE) + 1
     pl.semaphore_wait(barrier, ahead * beside - 1)
 
     def copy(n, i, j):
-        lo, hi = slots[j]
-        if j == 2:
-            src = lat.at[:, 1:2]
-        elif j == -2:
-            src = lat.at[:, 0:1]
-        else:
-            src = lat
+        lo, hi = {2: (2, 5), -2: (0, 3)}.get(j, (0, 5))
         return pltpu.make_async_remote_copy(
-            src_ref=src,
-            dst_ref=R.at[6 - 2 * i:8 - 2 * i, lo:hi],
+            src_ref=pack.at[lo:hi],
+            dst_ref=R.at[NBACK - i, 2 - j, lo:hi],
             send_sem=ssem.at[n],
             recv_sem=rsem.at[n],
             device_id=to(i, j),
@@ -90,6 +94,7 @@
             copy(n, i, j).start()
 
     WE[...] = jnp.zeros(WE.shape, BF)
+    loads[1].wait()
     for dc in range(3):
         for dt in range(3):
             for dr in range(3):
@@ -99,7 +104,7 @@
                         k = ((fo + dt) * 4 + ro + dr) * CI
                         n = (fo * 2 + ro) * C
                         WE[dc, k:k + CI, n:n + C] = w
-    load.wait()
+    loads[2].wait()
 
     def fold(s, carry):
         dt = s // 8
@@ -130,6 +135,7 @@
 
 def exchange(nt, nr, lat, ek, uk):
     vm = pl.BlockSpec(memory_space=pltpu.VMEM)
+    hbm = pl.BlockSpec(memory_space=pl.ANY)
     n = len(partners())
 
     def body(*refs):
@@ -138,28 +144,42 @@
     return pl.pallas_call(
         body,
         out_shape=(
-            jax.ShapeDtypeStruct((8, 8, CI, W), BF),
+            jax.ShapeDtypeStruct((4, 5, 5, CI, 128), BF),
             jax.ShapeDtypeStruct((3, 256, 1024), BF),
             jax.ShapeDtypeStruct((2, 2, 3, 2, 2, C, C), BF),
         ),
-        in_specs=[vm, vm, pl.BlockSpec(memory_space=pl.ANY)],
+        in_specs=[hbm, hbm, hbm],
         out_specs=(vm, vm, vm),
         scratch_shapes=[
+            pltpu.VMEM((2, 2, CI, W), BF),
+            pltpu.VMEM((3, 3, 3, CI, C), BF),
             pltpu.VMEM((3, 3, 3, C, C), BF),
-            pltpu.SemaphoreType.DMA,
+            pltpu.VMEM((5, CI, 128), BF),
+            pltpu.SemaphoreType.DMA((3,)),
             pltpu.SemaphoreType.DMA((n,)),
             pltpu.SemaphoreType.DMA((n,)),
         ],
         compiler_params=pltpu.CompilerParams(collective_id=0, has_side_effects=True, vmem_limit_bytes=16 * 2**20),
         name="exchange",
-    )(lat, ek, uk)
+    )(*[pltpu.with_memory_space_constraint(x, pltpu.HBM) for x in (lat, ek, uk)])
+
+
+def window(R, fp, g):
+    main, tail = [], []
+    for f in range(2):
+        for w in range(4):
+            b, r = ROW_OF[2 * g + w]
+            main.append(R[fp, b, 3 * r + f].astype(F32))
+            k = 32 * (2 * r + f)
+            tail.append(R[fp, b, 2].astype(F32)[:, k:k + 32])
+    return jnp.concatenate([jnp.concatenate(main, axis=0).T, jnp.concatenate(tail, axis=0).T], axis=0)
 
 
 def decode_body(n_rows, height, R, WE, W2, WU, out, V, B3, S3, I):
     row_base = lax.axis_index("rows") * height
     for g in range(3):
         for fp in range(4):
-            y = R[2 * fp:2 * fp + 2, 2 * g:2 * g + 4].reshape(128, W).astype(F32).T
+            y = window(R, fp, g)
             for d in range(3):
                 z = y if d == 1 else roll_cols(y, d)
                 V[d, g, fp] = z.astype(BF)
@@ -237,7 +257,7 @@
 def per_device(nt, nr, latent, entry_kernel, middle_kernel, upper_kernel):
     height = latent.shape[1]
     lat = jnp.transpose(latent, (0, 1, 3, 2))
-    R, WE, WU = exchange(nt, nr, lat, entry_kernel, pltpu.with_memory_space_constraint(upper_kernel, pltpu.HBM))
+    R, WE, WU = exchange(nt, nr, lat, entry_kernel, upper_kernel)
     return decode(height * nr, height, R, WE, middle_kernel, WU)
 
 

time: 38.8 us -> 35.1 us (0.905)
  the two profiles are of different devices: /device:TPU:28 before, /device:TPU:30 now
where the time goes in v2:
time: 35.1 us; the launch traced here: 35 us
  Pallas kernels  35 us (100%)
    pallas_call x1, Pallas kernels, decode(): pl.pallas_call(body, out_shape=jax.ShapeDtypeStruct((2, 4, 2 * W, C), BF)...  19.7 us
    pallas_call x1, Pallas kernels, exchange(): pl.pallas_call(body, out_shape=(jax.ShapeDtypeStruct((4, 5, 5, CI, 128),...  15.3 us

profile of v2, /device:TPU:30, one launch (start us, length us, event | category | flops | bytes accessed | tf_op | source)
XLA Modules:
  0.0 35.0 jit_solution(15127726636287413503)
XLA Ops:
  0.0 0.0 copy-start
  0.0 15.3 %exchange.1 = (bf16[4,5,5,16,128]{4,3,2,1,0:T(8,128)(2,1)S(1)}, bf16[3,256,1024]{2,1,0:T(8,128)(2,1)S(1)}, bf16[2,2,3,2,2,256,256]{6,5,4,3,2,1,0:T(8,128)(2,1)S(1)}) custom-call(bf16[2,2,16,160]{3,2,1,0:T(8,128)(2,1)} %bitcast.1, bf16[3,3,3,16,256]{4,3,2,1,0:T(8,128)(2,1)} %refs_1_.1, bf16[3,3,3,256,256]{4,3,2,1,0:T(8,128)(2,1)} %refs_2_.2), custom_call_target="tpu_custom_call" | custom-call | tf_op jit(solution)/shard_map/exchange/pallas_call | solution.py:144
  15.3 0.0 copy-done
  15.3 19.7 %decode.1 = bf16[2,4,320,256]{3,2,1,0:T(8,128)(2,1)} custom-call(bf16[4,5,5,16,128]{4,3,2,1,0:T(8,128)(2,1)S(1)} %get-tuple-element.8.refs_0_, bf16[3,256,1024]{2,1,0:T(8,128)(2,1)S(1)} %get-tuple-element.9.refs_1_, bf16[3,3,3,256,256]{4,3,2,1,0:T(8,128)(2,1)S(1)} %copy-done, bf16[2,2,3,2,2,256,256]{6,5,4,3,2,1,0:T(8,128)(2,1)S(1)} %get-tuple-element.10.refs_3_), custom_call_target="tpu_custom_call" | custom-call | tf_op jit(solution)/shard_map/decode/pallas_call | solution.py:241
Async XLA Ops:
  0.0 15.3 %copy-start = (bf16[3,3,3,256,256]{4,3,2,1,0:T(8,128)(2,1)S(1)}, bf16[3,3,3,256,256]{4,3,2,1,0:T(8,128)(2,1)}, u32[]{:S(2)}) copy-start(bf16[3,3,3,256,256]{4,3,2,1,0:T(8,128)(2,1)} %refs_2_.3) | copy-start | bytes 10616836

commit v3 on v2

--- a/solution.py
+++ b/solution.py
@@ -23,7 +23,8 @@
 
 
 def silu(v):
-    return v * (1.0 / (1.0 + jnp.exp(-v)))
+    h = 0.5 * v
+    return h + h * jnp.tanh(h)
 
 
 def put3(dst, idx, x):
@@ -39,7 +40,7 @@
 ROW_OF = ((0, 1), (1, 0), (1, 1), (2, 0), (2, 1), (3, 0), (3, 1), (4, 0))
 
 
-def exchange_body(nt, nr, lat_h, ek_h, uk, R, WE, WU, lat, ek, ubuf, pack, lsem, ssem, rsem):
+def exchange_body(nt, nr, lat_h, ek_h, uk, mk, R, WE, W2, WM, WU, lat, ek, ubuf, pack, lsem, ssem, rsem):
     me_t = lax.axis_index("tm")
     me_r = lax.axis_index("rows")
 
@@ -52,7 +53,7 @@
         return {"tm": me_t + di, "rows": me_r + dj}
 
     loads = [pltpu.make_async_copy(src, dst, lsem.at[n])
-             for n, (src, dst) in enumerate(((lat_h, lat), (ek_h, ek), (uk, ubuf)))]
+             for n, (src, dst) in enumerate(((lat_h, lat), (ek_h, ek), (uk, ubuf), (mk, W2)))]
     for x in loads:
         x.start()
     barrier = pltpu.get_barrier_semaphore()
@@ -88,7 +89,7 @@
             device_id_type=pl.DeviceIdType.MESH,
         )
 
-    for n, (i, j) in enumerate(partners()):
+    for n, (i, j) in reversed(list(enumerate(partners()))):
         @pl.when(there(i, j))
         def _():
             copy(n, i, j).start()
@@ -105,20 +106,26 @@
                         n = (fo * 2 + ro) * C
                         WE[dc, k:k + CI, n:n + C] = w
     loads[2].wait()
+    loads[3].wait()
 
     def fold(s, carry):
         dt = s // 8
         r0 = pl.multiple_of((s % 8) * 32, 32)
         m = [[ubuf[dt, r, c, pl.ds(r0, 32), :].astype(F32) for c in range(3)] for r in range(3)]
-        rows = [[m[0], [m[1][c] + m[2][c] for c in range(3)]],
-                [[m[0][c] + m[1][c] for c in range(3)], m[2]]]
-        for a in range(2):
-            for e in range(2):
-                q = rows[a][e]
-                cols = [[q[0], q[1] + q[2]], [q[0] + q[1], q[2]]]
-                for b in range(2):
-                    for c in range(2):
-                        WU[a, b, dt, e, c, pl.ds(r0, 32), :] = cols[b][c].astype(BF)
+        rows = [m[0], [m[0][c] + m[1][c] + m[2][c] for c in range(3)], m[2]]
+        for a in range(3):
+            q = rows[a]
+            cols = [[q[0], q[1] + q[2]], [q[0] + q[1], q[2]]]
+            for b in range(2):
+                for c in range(2):
+                    WU[a, b, dt, c, pl.ds(r0, 32), :] = cols[b][c].astype(BF)
+        dr = dt
+        for dc in range(3):
+            k = [W2[t, dr, dc, pl.ds(r0, 32), :].astype(F32) for t in range(3)]
+            half = 0.5 * (k[0] + k[2])
+            one = 0.5 * k[1]
+            WM[0, dr, dc, pl.ds(r0, 32), :] = (half + one).astype(BF)
+            WM[1, dr, dc, pl.ds(r0, 32), :] = (half - one).astype(BF)
         return carry
 
     lax.fori_loop(0, 24, fold, 0)
@@ -133,7 +140,7 @@
             copy(n, i, j).wait_recv()
 
 
-def exchange(nt, nr, lat, ek, uk):
+def exchange(nt, nr, lat, ek, uk, mk):
     vm = pl.BlockSpec(memory_space=pltpu.VMEM)
     hbm = pl.BlockSpec(memory_space=pl.ANY)
     n = len(partners())
@@ -146,22 +153,24 @@
         out_shape=(
             jax.ShapeDtypeStruct((4, 5, 5, CI, 128), BF),
             jax.ShapeDtypeStruct((3, 256, 1024), BF),
-            jax.ShapeDtypeStruct((2, 2, 3, 2, 2, C, C), BF),
+            jax.ShapeDtypeStruct((3, 3, 3, C, C), BF),
+            jax.ShapeDtypeStruct((2, 3, 3, C, C), BF),
+            jax.ShapeDtypeStruct((3, 2, 3, 2, C, C), BF),
         ),
-        in_specs=[hbm, hbm, hbm],
-        out_specs=(vm, vm, vm),
+        in_specs=[hbm] * 4,
+        out_specs=(vm,) * 5,
         scratch_shapes=[
             pltpu.VMEM((2, 2, CI, W), BF),
             pltpu.VMEM((3, 3, 3, CI, C), BF),
             pltpu.VMEM((3, 3, 3, C, C), BF),
             pltpu.VMEM((5, CI, 128), BF),
-            pltpu.SemaphoreType.DMA((3,)),
+            pltpu.SemaphoreType.DMA((4,)),
             pltpu.SemaphoreType.DMA((n,)),
             pltpu.SemaphoreType.DMA((n,)),
         ],
         compiler_params=pltpu.CompilerParams(collective_id=0, has_side_effects=True, vmem_limit_bytes=16 * 2**20),
         name="exchange",
-    )(*[pltpu.with_memory_space_constraint(x, pltpu.HBM) for x in (lat, ek, uk)])
+    )(*[pltpu.with_memory_space_constraint(x, pltpu.HBM) for x in (lat, ek, uk, mk)])
 
 
 def window(R, fp, g):
@@ -175,8 +184,15 @@
     return jnp.concatenate([jnp.concatenate(main, axis=0).T, jnp.concatenate(tail, axis=0).T], axis=0)
 
 
-def decode_body(n_rows, height, R, WE, W2, WU, out, V, B3, S3, I):
+FRAMES = ((0, 2, -1), (1, 2, 1), (2, 1, -1), (1, 3, -1))
+
+
+def decode_body(n_rows, height, R, WE, W2, WM, WU, out, V, B3, S3, I, CR, MID):
     row_base = lax.axis_index("rows") * height
+
+    def inside(r):
+        return jnp.where((r >= 0) & (r < n_rows), 1.0, 0.0)
+
     for g in range(3):
         for fp in range(4):
             y = window(R, fp, g)
@@ -192,38 +208,57 @@
                 p = jnp.dot(lhs, WE[d, :, fo * 512:(fo + 1) * 512], preferred_element_type=F32)
                 acc = p if acc is None else acc + p
             for ro in range(2):
-                gr = row_base - 2 + 2 * g + ro
-                ok = jnp.where((gr >= 0) & (gr < n_rows), 1.0, 0.0)
+                ok = inside(row_base - 2 + 2 * g + ro)
                 for k in range(3):
                     put3(B3, (2 * k + fo, 2 * g + ro), acc[k * W:(k + 1) * W, ro * C:(ro + 1) * C] * ok)
 
-    def mid(f, carry):
+    for p in range(2):
+        f0 = 2 * p
+        for i in range(4):
+            fa, fb, sign = FRAMES[i]
+            acc = None
+            for dr in range(3):
+                for dc in range(3):
+                    u = B3[dc, f0 + fa, dr:dr + 4].reshape(4 * W, C)
+                    v = B3[dc, f0 + fb, dr:dr + 4].reshape(4 * W, C)
+                    lhs = u + v if sign > 0 else u - v
+                    w = W2[0, dr, dc] if i == 0 else W2[2, dr, dc] if i == 3 else WM[i - 1, dr, dc]
+                    q = jnp.dot(lhs, w, preferred_element_type=F32)
+                    acc = q if acc is None else acc + q
+            if i == 0:
+                MID[0] = acc
+            elif i == 1:
+                MID[0] = MID[0] + acc
+                MID[1] = acc
+            else:
+                t = i - 2
+                if t == 0:
+                    y = MID[0] + acc
+                    MID[1] = MID[1] - acc
+                else:
+                    y = MID[1] - acc
+                for r in range(4):
+                    s = (B3[1, f0 + t + 2, r + 1].astype(F32) + silu(y[r * W:(r + 1) * W])) * inside(row_base - 1 + r)
+                    put3(S3, (f0 + t, r), s)
+
+    def prod(a, b):
         acc = None
         for dt in range(3):
-            for dr in range(3):
-                for dc in range(3):
-                    lhs = B3[dc, f + dt, dr:dr + 4].reshape(4 * W, C)
-                    p = jnp.dot(lhs, W2[dt, dr, dc], preferred_element_type=F32)
-                    acc = p if acc is None else acc + p
-        for r in range(4):
-            gr = row_base - 1 + r
-            ok = jnp.where((gr >= 0) & (gr < n_rows), 1.0, 0.0)
-            s = (B3[1, f + 2, r + 1].astype(F32) + silu(acc[r * W:(r + 1) * W])) * ok
-            put3(S3, (f, r), s)
-        return carry
-
-    lax.fori_loop(0, 4, mid, 0)
+            for c in range(2):
+                parts = []
+                for t in range(2):
+                    for q in range(2):
+                        x = [S3[b + c, t + dt, q + k] for k in ((0, 1), (1,), (1, 2))[a]]
+                        parts.append(x[0] if a == 1 else x[0] - x[1] if a == 0 else x[1] - x[0])
+                p = jnp.dot(jnp.concatenate(parts, axis=0), WU[a, b, dt, c], preferred_element_type=F32)
+                acc = p if acc is None else acc + p
+        return acc
+
+    for b in range(2):
+        CR[b] = prod(1, b)
     for a in range(2):
         for b in range(2):
-            acc = None
-            for dt in range(3):
-                for e in range(2):
-                    for c in range(2):
-                        lhs = jnp.concatenate(
-                            [S3[b + c, t + dt, a + e + q] for t in range(2) for q in range(2)], axis=0)
-                        p = jnp.dot(lhs, WU[a, b, dt, e, c], preferred_element_type=F32)
-                        acc = p if acc is None else acc + p
-            y = silu(acc)
+            y = silu(prod(2 * a, b) + CR[b])
             for i in range(4):
                 for h in range(2):
                     I[i, h, pl.ds(b, W, stride=2), :] = y[i * W:(i + 1) * W, h * 128:(h + 1) * 128]
@@ -232,7 +267,7 @@
                 out[i // 2, 2 * (i % 2) + a, :, h * 128:(h + 1) * 128] = I[i, h].astype(BF)
 
 
-def decode(n_rows, height, R, WE, W2, WU):
+def decode(n_rows, height, *operands):
     vm = pl.BlockSpec(memory_space=pltpu.VMEM)
 
     def body(*refs):
@@ -241,24 +276,25 @@
     return pl.pallas_call(
         body,
         out_shape=jax.ShapeDtypeStruct((2, 4, 2 * W, C), BF),
-        in_specs=[vm, vm, vm, vm],
+        in_specs=[vm] * len(operands),
         out_specs=vm,
         scratch_shapes=[
             pltpu.VMEM((3, 3, 4, W, 128), BF),
             pltpu.VMEM((3, 6, 6, W, C), BF),
             pltpu.VMEM((3, 4, 4, W, C), BF),
             pltpu.VMEM((4, 2, 2 * W, 128), F32),
+            pltpu.VMEM((2, 4 * W, C), F32),
+            pltpu.VMEM((2, 4 * W, C), F32),
         ],
-        compiler_params=pltpu.CompilerParams(vmem_limit_bytes=40 * 2**20),
+        compiler_params=pltpu.CompilerParams(vmem_limit_bytes=32 * 2**20),
         name="decode",
-    )(R, WE, W2, WU)
+    )(*operands)
 
 
 def per_device(nt, nr, latent, entry_kernel, middle_kernel, upper_kernel):
     height = latent.shape[1]
     lat = jnp.transpose(latent, (0, 1, 3, 2))
-    R, WE, WU = exchange(nt, nr, lat, entry_kernel, upper_kernel)
-    return decode(height * nr, height, R, WE, middle_kernel, WU)
+    return decode(height * nr, height, *exchange(nt, nr, lat, entry_kernel, upper_kernel, middle_kernel))
 
 
 def solution(mesh):

time: 35.1 us -> 29.4 us (0.84)
  the two profiles are of different devices: /device:TPU:30 before, /device:TPU:1 now
where the time goes in v3:
time: 29.4 us; the launch traced here: 29.3 us
  Pallas kernels  29.3 us (100%)
    pallas_call x1, Pallas kernels, exchange(): pl.pallas_call(body, out_shape=(jax.ShapeDtypeStruct((4, 5, 5, CI, 128),...  15.3 us
    pallas_call x1, Pallas kernels, decode(): pl.pallas_call(body, out_shape=jax.ShapeDtypeStruct((2, 4, 2 * W, C), BF)...  14 us

profile of v3, /device:TPU:1, one launch (start us, length us, event | category | flops | bytes accessed | tf_op | source)
XLA Modules:
  0.0 29.3 jit_solution(14143757851690251729)
XLA Ops:
  0.0 15.3 %exchange.1 = (bf16[4,5,5,16,128]{4,3,2,1,0:T(8,128)(2,1)S(1)}, bf16[3,256,1024]{2,1,0:T(8,128)(2,1)S(1)}, bf16[3,3,3,256,256]{4,3,2,1,0:T(8,128)(2,1)S(1)}, bf1...) custom-call(bf16[2,2,16,160]{3,2,1,0:T(8,128)(2,1)} %bitcast.1, ...), custom_call_target="tpu_custom_call" | custom-call | tf_op jit(solution)/shard_map/exchange/pallas_call | solution.py:151
  15.3 14.0 %decode.1 = bf16[2,4,320,256]{3,2,1,0:T(8,128)(2,1)} custom-call(bf16[4,5,5,16,128]{4,3,2,1,0:T(8,128)(2,1)S(1)} %get-tuple-element.10.refs_0_, bf16[3,256,1024]{2,1,0:T(8,128)(2,1)S(1)} %get-tuple-element.11.refs_1_, bf16[3,3,3,256,256]{4,3,2,1,0:T(8,128)(2,1)S(1)} %get-tuple-element.12.refs_2_, bf16[2,3,3,256,256]{4,3,2,1,0:T(8,128)(2,1)S(1)} %get-tuple-element.13.refs_3_, ...), custom_call_target="tpu_custom_call" | custom-call | tf_op jit(solution)/shard_map/decode/pallas_call | solution.py:276

commit v4 on v3

--- a/solution.py
+++ b/solution.py
@@ -40,7 +40,7 @@
 ROW_OF = ((0, 1), (1, 0), (1, 1), (2, 0), (2, 1), (3, 0), (3, 1), (4, 0))
 
 
-def exchange_body(nt, nr, lat_h, ek_h, uk, mk, R, WE, W2, WM, WU, lat, ek, ubuf, pack, lsem, ssem, rsem):
+def section_body(nt, nr, height, lat_h, ek_h, uk, mk, out, R, WE, W2, WM, WU, V, B3, S3, I, CR, MID, lat, ek, ubuf, pack, lsem, ssem, rsem):
     me_t = lax.axis_index("tm")
     me_r = lax.axis_index("rows")
 
@@ -89,7 +89,7 @@
             device_id_type=pl.DeviceIdType.MESH,
         )
 
-    for n, (i, j) in reversed(list(enumerate(partners()))):
+    for n, (i, j) in enumerate(partners()):
         @pl.when(there(i, j))
         def _():
             copy(n, i, j).start()
@@ -130,47 +130,34 @@
 
     lax.fori_loop(0, 24, fold, 0)
 
+    def arrived(back):
+        for n, (i, j) in enumerate(partners()):
+            if i == back:
+                @pl.when(there(-i, -j))
+                def _():
+                    copy(n, i, j).wait_recv()
+
+    row_base = me_r * height
+    n_rows = nr * height
+    arrived(0)
+    arrived(1)
+    entry(row_base, n_rows, 2, (2, 3), R, WE, V, B3)
+    arrived(2)
+    entry(row_base, n_rows, 1, (1,), R, WE, V, B3)
+    middle(row_base, n_rows, 1, W2, WM, B3, S3, MID)
+    arrived(3)
+    entry(row_base, n_rows, 0, (0,), R, WE, V, B3)
+    middle(row_base, n_rows, 0, W2, WM, B3, S3, MID)
+    upper(WU, S3, I, CR, out)
+
     for n, (i, j) in enumerate(partners()):
         @pl.when(there(i, j))
         def _():
             copy(n, i, j).wait_send()
 
-        @pl.when(there(-i, -j))
-        def _():
-            copy(n, i, j).wait_recv()
-
-
-def exchange(nt, nr, lat, ek, uk, mk):
-    vm = pl.BlockSpec(memory_space=pltpu.VMEM)
-    hbm = pl.BlockSpec(memory_space=pl.ANY)
-    n = len(partners())
-
-    def body(*refs):
-        exchange_body(nt, nr, *refs)
-
-    return pl.pallas_call(
-        body,
-        out_shape=(
-            jax.ShapeDtypeStruct((4, 5, 5, CI, 128), BF),
-            jax.ShapeDtypeStruct((3, 256, 1024), BF),
-            jax.ShapeDtypeStruct((3, 3, 3, C, C), BF),
-            jax.ShapeDtypeStruct((2, 3, 3, C, C), BF),
-            jax.ShapeDtypeStruct((3, 2, 3, 2, C, C), BF),
-        ),
-        in_specs=[hbm] * 4,
-        out_specs=(vm,) * 5,
-        scratch_shapes=[
-            pltpu.VMEM((2, 2, CI, W), BF),
-            pltpu.VMEM((3, 3, 3, CI, C), BF),
-            pltpu.VMEM((3, 3, 3, C, C), BF),
-            pltpu.VMEM((5, CI, 128), BF),
-            pltpu.SemaphoreType.DMA((4,)),
-            pltpu.SemaphoreType.DMA((n,)),
-            pltpu.SemaphoreType.DMA((n,)),
-        ],
-        compiler_params=pltpu.CompilerParams(collective_id=0, has_side_effects=True, vmem_limit_bytes=16 * 2**20),
-        name="exchange",
-    )(*[pltpu.with_memory_space_constraint(x, pltpu.HBM) for x in (lat, ek, uk, mk)])
+
+def inside(r, n_rows):
+    return jnp.where((r >= 0) & (r < n_rows), 1.0, 0.0)
 
 
 def window(R, fp, g):
@@ -187,60 +174,58 @@
 FRAMES = ((0, 2, -1), (1, 2, 1), (2, 1, -1), (1, 3, -1))
 
 
-def decode_body(n_rows, height, R, WE, W2, WM, WU, out, V, B3, S3, I, CR, MID):
-    row_base = lax.axis_index("rows") * height
-
-    def inside(r):
-        return jnp.where((r >= 0) & (r < n_rows), 1.0, 0.0)
-
+def entry(row_base, n_rows, k, new, R, WE, V, B3):
     for g in range(3):
-        for fp in range(4):
+        for fp in new:
             y = window(R, fp, g)
             for d in range(3):
                 z = y if d == 1 else roll_cols(y, d)
                 V[d, g, fp] = z.astype(BF)
-    for g in range(3):
-        for fo in range(2):
-            acc = None
-            for d in range(3):
-                lhs = jnp.concatenate(
-                    [jnp.concatenate([V[d, g, k], V[d, g, k + 1]], axis=1) for k in range(3)], axis=0)
-                p = jnp.dot(lhs, WE[d, :, fo * 512:(fo + 1) * 512], preferred_element_type=F32)
-                acc = p if acc is None else acc + p
+    for fo in range(2):
+        acc = None
+        for d in range(3):
+            lhs = jnp.concatenate(
+                [jnp.concatenate([V[d, g, k], V[d, g, k + 1]], axis=1) for g in range(3)], axis=0)
+            p = jnp.dot(lhs, WE[d, :, fo * 512:(fo + 1) * 512], preferred_element_type=F32)
+            acc = p if acc is None else acc + p
+        for g in range(3):
             for ro in range(2):
-                ok = inside(row_base - 2 + 2 * g + ro)
-                for k in range(3):
-                    put3(B3, (2 * k + fo, 2 * g + ro), acc[k * W:(k + 1) * W, ro * C:(ro + 1) * C] * ok)
-
-    for p in range(2):
-        f0 = 2 * p
-        for i in range(4):
-            fa, fb, sign = FRAMES[i]
-            acc = None
-            for dr in range(3):
-                for dc in range(3):
-                    u = B3[dc, f0 + fa, dr:dr + 4].reshape(4 * W, C)
-                    v = B3[dc, f0 + fb, dr:dr + 4].reshape(4 * W, C)
-                    lhs = u + v if sign > 0 else u - v
-                    w = W2[0, dr, dc] if i == 0 else W2[2, dr, dc] if i == 3 else WM[i - 1, dr, dc]
-                    q = jnp.dot(lhs, w, preferred_element_type=F32)
-                    acc = q if acc is None else acc + q
-            if i == 0:
-                MID[0] = acc
-            elif i == 1:
-                MID[0] = MID[0] + acc
-                MID[1] = acc
+                ok = inside(row_base - 2 + 2 * g + ro, n_rows)
+                put3(B3, (2 * k + fo, 2 * g + ro), acc[g * W:(g + 1) * W, ro * C:(ro + 1) * C] * ok)
+
+
+def middle(row_base, n_rows, p, W2, WM, B3, S3, MID):
+    f0 = 2 * p
+    for i in range(4):
+        fa, fb, sign = FRAMES[i]
+        acc = None
+        for dr in range(3):
+            for dc in range(3):
+                u = B3[dc, f0 + fa, dr:dr + 4].reshape(4 * W, C)
+                v = B3[dc, f0 + fb, dr:dr + 4].reshape(4 * W, C)
+                lhs = u + v if sign > 0 else u - v
+                w = W2[0, dr, dc] if i == 0 else W2[2, dr, dc] if i == 3 else WM[i - 1, dr, dc]
+                q = jnp.dot(lhs, w, preferred_element_type=F32)
+                acc = q if acc is None else acc + q
+        if i == 0:
+            MID[0] = acc
+        elif i == 1:
+            MID[0] = MID[0] + acc
+            MID[1] = acc
+        else:
+            t = i - 2
+            if t == 0:
+                y = MID[0] + acc
+                MID[1] = MID[1] - acc
             else:
-                t = i - 2
-                if t == 0:
-                    y = MID[0] + acc
-                    MID[1] = MID[1] - acc
-                else:
-                    y = MID[1] - acc
-                for r in range(4):
-                    s = (B3[1, f0 + t + 2, r + 1].astype(F32) + silu(y[r * W:(r + 1) * W])) * inside(row_base - 1 + r)
-                    put3(S3, (f0 + t, r), s)
-
+                y = MID[1] - acc
+            for r in range(4):
+                ok = inside(row_base - 1 + r, n_rows)
+                s = (B3[1, f0 + t + 2, r + 1].astype(F32) + silu(y[r * W:(r + 1) * W])) * ok
+                put3(S3, (f0 + t, r), s)
+
+
+def upper(WU, S3, I, CR, out):
     def prod(a, b):
         acc = None
         for dt in range(3):
@@ -267,34 +252,45 @@
                 out[i // 2, 2 * (i % 2) + a, :, h * 128:(h + 1) * 128] = I[i, h].astype(BF)
 
 
-def decode(n_rows, height, *operands):
-    vm = pl.BlockSpec(memory_space=pltpu.VMEM)
+def section(nt, nr, height, *operands):
+    n = len(partners())
 
     def body(*refs):
-        decode_body(n_rows, height, *refs)
+        section_body(nt, nr, height, *refs)
 
     return pl.pallas_call(
         body,
         out_shape=jax.ShapeDtypeStruct((2, 4, 2 * W, C), BF),
-        in_specs=[vm] * len(operands),
-        out_specs=vm,
+        in_specs=[pl.BlockSpec(memory_space=pl.ANY)] * 4,
+        out_specs=pl.BlockSpec(memory_space=pltpu.VMEM),
         scratch_shapes=[
+            pltpu.VMEM((4, 5, 5, CI, 128), BF),
+            pltpu.VMEM((3, 256, 1024), BF),
+            pltpu.VMEM((3, 3, 3, C, C), BF),
+            pltpu.VMEM((2, 3, 3, C, C), BF),
+            pltpu.VMEM((3, 2, 3, 2, C, C), BF),
             pltpu.VMEM((3, 3, 4, W, 128), BF),
             pltpu.VMEM((3, 6, 6, W, C), BF),
             pltpu.VMEM((3, 4, 4, W, C), BF),
             pltpu.VMEM((4, 2, 2 * W, 128), F32),
             pltpu.VMEM((2, 4 * W, C), F32),
             pltpu.VMEM((2, 4 * W, C), F32),
+            pltpu.VMEM((2, 2, CI, W), BF),
+            pltpu.VMEM((3, 3, 3, CI, C), BF),
+            pltpu.VMEM((3, 3, 3, C, C), BF),
+            pltpu.VMEM((5, CI, 128), BF),
+            pltpu.SemaphoreType.DMA((4,)),
+            pltpu.SemaphoreType.DMA((n,)),
+            pltpu.SemaphoreType.DMA((n,)),
         ],
-        compiler_params=pltpu.CompilerParams(vmem_limit_bytes=32 * 2**20),
-        name="decode",
-    )(*operands)
+        compiler_params=pltpu.CompilerParams(collective_id=0, has_side_effects=True, vmem_limit_bytes=46 * 2**20),
+        name="section",
+    )(*[pltpu.with_memory_space_constraint(x, pltpu.HBM) for x in operands])
 
 
 def per_device(nt, nr, latent, entry_kernel, middle_kernel, upper_kernel):
-    height = latent.shape[1]
     lat = jnp.transpose(latent, (0, 1, 3, 2))
-    return decode(height * nr, height, *exchange(nt, nr, lat, entry_kernel, upper_kernel, middle_kernel))
+    return section(nt, nr, latent.shape[1], lat, entry_kernel, upper_kernel, middle_kernel)
 
 
 def solution(mesh):

time: 29.4 us -> 29.9 us (1.017)
  the two profiles are of different devices: /device:TPU:1 before, /device:TPU:26 now
where the time goes in v4:
time: 29.9 us; the launch traced here: 29.8 us
  Pallas kernels  28.8 us (96%)
  local copies, waits for them, and re-layouts  1.06 us (4%)
    pallas_call x1, Pallas kernels, section(): pl.pallas_call(body, out_shape=jax.ShapeDtypeStruct((2, 4, 2 * W, C), BF)...  28.8 us
    unnamed x1, local copies, waits for them, and re-layouts  1.06 us

profile of v4, /device:TPU:26, one launch (start us, length us, event | category | flops | bytes accessed | tf_op | source)
XLA Modules:
  0.0 29.8 jit_solution(840673526261814506)
XLA Ops:
  0.0 28.8 %section.1 = bf16[2,4,320,256]{3,2,1,0:T(8,128)(2,1)S(1)} custom-call(bf16[2,2,16,160]{3,2,1,0:T(8,128)(2,1)} %bitcast.1, bf16[3,3,3,16,256]{4,3,2,1,0:T(8,128)(2,1)} %refs_1_.1, bf16[3,3,3,256,256]{4,3,2,1,0:T(8,128)(2,1)} %refs_2_.1, bf16[3,3,3,256,256]{4,3,2,1,0:T(8,128)(2,1)} %refs_3_.1), custom_call_target="tpu_custom_call" | custom-call | tf_op jit(solution)/shard_map/section/pallas_call | solution.py:261
  28.8 1.1 %copy.6 = bf16[2,4,320,256]{3,2,1,0:T(8,128)(2,1)} copy(bf16[2,4,320,256]{3,2,1,0:T(8,128)(2,1)S(1)} %section.1) | data formatting | bytes 2621440

commit v5 on v3

--- a/solution.py
+++ b/solution.py
@@ -33,6 +33,12 @@
         dst[(d,) + idx] = y.astype(BF)
 
 
+def four(g):
+    half = 0.5 * (g[0] + g[2])
+    one = 0.5 * g[1]
+    return [g[0], half + one, half - one, g[2]]
+
+
 def partners():
     return [(i, j) for i in range(NBACK + 1) for j in range(-NSIDE, NSIDE + 1) if (i, j) != (0, 0)]
 
@@ -40,7 +46,7 @@
 ROW_OF = ((0, 1), (1, 0), (1, 1), (2, 0), (2, 1), (3, 0), (3, 1), (4, 0))
 
 
-def exchange_body(nt, nr, lat_h, ek_h, uk, mk, R, WE, W2, WM, WU, lat, ek, ubuf, pack, lsem, ssem, rsem):
+def exchange_body(nt, nr, lat_h, ek_h, uk, mk, R, WE, WM, WU, lat, ek, ubuf, mbuf, pack, lsem, ssem, rsem):
     me_t = lax.axis_index("tm")
     me_r = lax.axis_index("rows")
 
@@ -53,7 +59,7 @@
         return {"tm": me_t + di, "rows": me_r + dj}
 
     loads = [pltpu.make_async_copy(src, dst, lsem.at[n])
-             for n, (src, dst) in enumerate(((lat_h, lat), (ek_h, ek), (uk, ubuf), (mk, W2)))]
+             for n, (src, dst) in enumerate(((lat_h, lat), (ek_h, ek), (uk, ubuf), (mk, mbuf)))]
     for x in loads:
         x.start()
     barrier = pltpu.get_barrier_semaphore()
@@ -119,13 +125,13 @@
             for b in range(2):
                 for c in range(2):
                     WU[a, b, dt, c, pl.ds(r0, 32), :] = cols[b][c].astype(BF)
-        dr = dt
-        for dc in range(3):
-            k = [W2[t, dr, dc, pl.ds(r0, 32), :].astype(F32) for t in range(3)]
-            half = 0.5 * (k[0] + k[2])
-            one = 0.5 * k[1]
-            WM[0, dr, dc, pl.ds(r0, 32), :] = (half + one).astype(BF)
-            WM[1, dr, dc, pl.ds(r0, 32), :] = (half - one).astype(BF)
+        dc = dt
+        k = [[mbuf[t, r, dc, pl.ds(r0, 32), :].astype(F32) for r in range(3)] for t in range(3)]
+        cols = [four([k[t][r] for t in range(3)]) for r in range(3)]
+        for i in range(4):
+            w = four([cols[r][i] for r in range(3)])
+            for j in range(4):
+                WM[i, j, dc, pl.ds(r0, 32), :] = w[j].astype(BF)
         return carry
 
     lax.fori_loop(0, 24, fold, 0)
@@ -153,15 +159,15 @@
         out_shape=(
             jax.ShapeDtypeStruct((4, 5, 5, CI, 128), BF),
             jax.ShapeDtypeStruct((3, 256, 1024), BF),
-            jax.ShapeDtypeStruct((3, 3, 3, C, C), BF),
-            jax.ShapeDtypeStruct((2, 3, 3, C, C), BF),
+            jax.ShapeDtypeStruct((4, 4, 3, C, C), BF),
             jax.ShapeDtypeStruct((3, 2, 3, 2, C, C), BF),
         ),
         in_specs=[hbm] * 4,
-        out_specs=(vm,) * 5,
+        out_specs=(vm,) * 4,
         scratch_shapes=[
             pltpu.VMEM((2, 2, CI, W), BF),
             pltpu.VMEM((3, 3, 3, CI, C), BF),
+            pltpu.VMEM((3, 3, 3, C, C), BF),
             pltpu.VMEM((3, 3, 3, C, C), BF),
             pltpu.VMEM((5, CI, 128), BF),
             pltpu.SemaphoreType.DMA((4,)),
@@ -184,10 +190,10 @@
     return jnp.concatenate([jnp.concatenate(main, axis=0).T, jnp.concatenate(tail, axis=0).T], axis=0)
 
 
-FRAMES = ((0, 2, -1), (1, 2, 1), (2, 1, -1), (1, 3, -1))
-
-
-def decode_body(n_rows, height, R, WE, W2, WM, WU, out, V, B3, S3, I, CR, MID):
+PAIRS = ((0, 2, -1), (1, 2, 1), (2, 1, -1), (1, 3, -1))
+
+
+def decode_body(n_rows, height, R, WE, WM, WU, out_h, out, V, B3, S3, I, CR, MID, Y, osem):
     row_base = lax.axis_index("rows") * height
 
     def inside(r):
@@ -212,38 +218,55 @@
                 for k in range(3):
                     put3(B3, (2 * k + fo, 2 * g + ro), acc[k * W:(k + 1) * W, ro * C:(ro + 1) * C] * ok)
 
-    for p in range(2):
-        f0 = 2 * p
-        for i in range(4):
-            fa, fb, sign = FRAMES[i]
-            acc = None
-            for dr in range(3):
-                for dc in range(3):
-                    u = B3[dc, f0 + fa, dr:dr + 4].reshape(4 * W, C)
-                    v = B3[dc, f0 + fb, dr:dr + 4].reshape(4 * W, C)
-                    lhs = u + v if sign > 0 else u - v
-                    w = W2[0, dr, dc] if i == 0 else W2[2, dr, dc] if i == 3 else WM[i - 1, dr, dc]
-                    q = jnp.dot(lhs, w, preferred_element_type=F32)
-                    acc = q if acc is None else acc + q
+    def product(i, j):
+        fa, fb, fs = PAIRS[i]
+        ra, rb, rs = PAIRS[j]
+        acc = None
+        for dc in range(3):
+            parts = []
+            for p in range(2):
+                for q in range(2):
+                    x = [B3[dc, 2 * p + f, 2 * q + r] for f in (fa, fb) for r in (ra, rb)]
+                    u, v = (x[0] + x[1], x[2] + x[3]) if rs > 0 else (x[0] - x[1], x[2] - x[3])
+                    parts.append(u + v if fs > 0 else u - v)
+            z = jnp.dot(jnp.concatenate(parts, axis=0), WM[i, j, dc], preferred_element_type=F32)
+            acc = z if acc is None else acc + z
+        return acc
+
+    def finish(t, h, y):
+        for p in range(2):
+            for q in range(2):
+                r = 2 * q + h
+                m = (2 * p + q) * W
+                s = (B3[1, 2 * p + t + 2, r + 1].astype(F32) + silu(y[m:m + W])) * inside(row_base - 1 + r)
+                put3(S3, (2 * p + t, r), s)
+
+    for i in range(4):
+        MID[0] = product(i, 0)
+        x = product(i, 1)
+        MID[0] = MID[0] + x
+        MID[1] = x
+        for h in range(2):
+            if h == 0:
+                x = product(i, 2)
+                z = MID[0] + x
+                MID[1] = MID[1] - x
+            else:
+                z = MID[1] - product(i, 3)
             if i == 0:
-                MID[0] = acc
+                Y[0, h] = z
             elif i == 1:
-                MID[0] = MID[0] + acc
-                MID[1] = acc
+                Y[0, h] = Y[0, h] + z
+                Y[1, h] = z
+            elif i == 2:
+                finish(0, h, Y[0, h] + z)
+                Y[1, h] = Y[1, h] - z
             else:
-                t = i - 2
-                if t == 0:
-                    y = MID[0] + acc
-                    MID[1] = MID[1] - acc
-                else:
-                    y = MID[1] - acc
-                for r in range(4):
-                    s = (B3[1, f0 + t + 2, r + 1].astype(F32) + silu(y[r * W:(r + 1) * W])) * inside(row_base - 1 + r)
-                    put3(S3, (f0 + t, r), s)
+                finish(1, h, Y[1, h] - z)
 
     def prod(a, b):
         acc = None
-        for dt in range(3):
+        for dt in (2, 1, 0):
             for c in range(2):
                 parts = []
                 for t in range(2):
@@ -253,6 +276,10 @@
                 p = jnp.dot(jnp.concatenate(parts, axis=0), WU[a, b, dt, c], preferred_element_type=F32)
                 acc = p if acc is None else acc + p
         return acc
+
+    def store(a, i):
+        at = (i // 2, 2 * (i % 2) + a)
+        return pltpu.make_async_copy(out.at[at], out_h.at[at], osem.at[4 * a + i])
 
     for b in range(2):
         CR[b] = prod(1, b)
@@ -265,6 +292,10 @@
         for i in range(4):
             for h in range(2):
                 out[i // 2, 2 * (i % 2) + a, :, h * 128:(h + 1) * 128] = I[i, h].astype(BF)
+            store(a, i).start()
+    for a in range(2):
+        for i in range(4):
+            store(a, i).wait()
 
 
 def decode(n_rows, height, *operands):
@@ -277,14 +308,17 @@
         body,
         out_shape=jax.ShapeDtypeStruct((2, 4, 2 * W, C), BF),
         in_specs=[vm] * len(operands),
-        out_specs=vm,
+        out_specs=pl.BlockSpec(memory_space=pl.ANY),
         scratch_shapes=[
+            pltpu.VMEM((2, 4, 2 * W, C), BF),
             pltpu.VMEM((3, 3, 4, W, 128), BF),
             pltpu.VMEM((3, 6, 6, W, C), BF),
             pltpu.VMEM((3, 4, 4, W, C), BF),
             pltpu.VMEM((4, 2, 2 * W, 128), F32),
             pltpu.VMEM((2, 4 * W, C), F32),
             pltpu.VMEM((2, 4 * W, C), F32),
+            pltpu.VMEM((2, 2, 4 * W, C), F32),
+            pltpu.SemaphoreType.DMA((8,)),
         ],
         compiler_params=pltpu.CompilerParams(vmem_limit_bytes=32 * 2**20),
         name="decode",

time: 29.4 us -> 27.7 us (0.942)
  Pallas kernels: 29.3 us -> 27.6 us
    pallas_call x1, Pallas kernels: 14 us -> 12.3 us  [decode(): pl.pallas_call(body, out_shape=jax.ShapeDtypeStruct((2, 4, 2 * W, C), BF)...]
where the time goes in v5:
time: 27.7 us; the launch traced here: 27.6 us
  Pallas kernels  27.6 us (100%)
    pallas_call x1, Pallas kernels, exchange(): pl.pallas_call(body, out_shape=(jax.ShapeDtypeStruct((4, 5, 5, CI, 128),...  15.3 us
    pallas_call x1, Pallas kernels, decode(): pl.pallas_call(body, out_shape=jax.ShapeDtypeStruct((2, 4, 2 * W, C), BF)...  12.3 us

profile of v5, /device:TPU:1, one launch (start us, length us, event | category | flops | bytes accessed | tf_op | source)
XLA Modules:
  0.0 27.6 jit_solution(2395719143675285346)
XLA Ops:
  0.0 15.3 %exchange.1 = (bf16[4,5,5,16,128]{4,3,2,1,0:T(8,128)(2,1)S(1)}, bf16[3,256,1024]{2,1,0:T(8,128)(2,1)S(1)}, bf16[4,4,3,256,256]{4,3,2,1,0:T(8,128)(2,1)S(1)}, bf16[3,2,3,2,256,256]{5,4,3,2,1,0:T(8,128)(2,1)S(1)}) custom-call(bf16[2,2,16,160]{3,2,1,0:T(8,128)(2,1)} %bitcast.1, bf16[3,3,3,16,256]{4,3,2,1,0:T(8,128)(2,1)} %refs_1_.1, ...), custom_call_target="tpu_custom_call" | custom-call | tf_op jit(solution)/shard_map/exchange/pallas_call | solution.py:157
  15.3 12.3 %decode.1 = bf16[2,4,320,256]{3,2,1,0:T(8,128)(2,1)} custom-call(bf16[4,5,5,16,128]{4,3,2,1,0:T(8,128)(2,1)S(1)} %get-tuple-element.9.refs_0_, bf16[3,256,1024]{2,1,0:T(8,128)(2,1)S(1)} %get-tuple-element.10.refs_1_, bf16[4,4,3,256,256]{4,3,2,1,0:T(8,128)(2,1)S(1)} %get-tuple-element.11.refs_2_, bf16[3,2,3,2,256,256]{5,4,3,2,1,0:T(8,128)(2,1)S(1)} %get-tuple-element.12.refs_3_), custom_call_target="tpu_custom_call" | custom-call | tf_op jit(solution)/shard_map/decode/pallas_call | solution.py:307

commit v6 on v5

--- a/solution.py
+++ b/solution.py
@@ -12,6 +12,7 @@
 CI = 16
 NBACK = 3
 NSIDE = 2
+ORDER = (2, 1, 3, 0)
 
 
 def roll_cols(x, d):
@@ -46,7 +47,7 @@
 ROW_OF = ((0, 1), (1, 0), (1, 1), (2, 0), (2, 1), (3, 0), (3, 1), (4, 0))
 
 
-def exchange_body(nt, nr, lat_h, ek_h, uk, mk, R, WE, WM, WU, lat, ek, ubuf, mbuf, pack, lsem, ssem, rsem):
+def exchange_body(nt, nr, lat_h, ek_h, uk, mk, R, WE, WM, WU, lat, ek, ubuf, mbuf, pack, lsem, ssem, rsem, fsem):
     me_t = lax.axis_index("tm")
     me_r = lax.axis_index("rows")
 
@@ -57,6 +58,15 @@
 
     def to(di, dj):
         return {"tm": me_t + di, "rows": me_r + dj}
+
+    even = lax.rem(me_t, 2) == 0
+    odd = lax.rem(me_t, 2) == 1
+
+    def sends(i, j):
+        return there(i, j) & even if i == 2 else there(i, j) & odd if i == 3 else there(i, j)
+
+    def gets(i, j):
+        return there(-i, -j) & even if i >= 2 else there(-i, -j)
 
     loads = [pltpu.make_async_copy(src, dst, lsem.at[n])
              for n, (src, dst) in enumerate(((lat_h, lat), (ek_h, ek), (uk, ubuf), (mk, mbuf)))]
@@ -64,7 +74,7 @@
         x.start()
     barrier = pltpu.get_barrier_semaphore()
     for i, j in partners():
-        @pl.when(there(-i, -j))
+        @pl.when(gets(i, j))
         def _():
             pl.semaphore_signal(barrier, inc=1, device_id=to(-i, -j), device_id_type=pl.DeviceIdType.MESH)
     for i, j in partners():
@@ -80,7 +90,8 @@
             tails.append(v[:, 128:].astype(F32))
     pack[2] = jnp.concatenate(tails, axis=1).astype(BF)
     R[NBACK, 2] = pack[...]
-    ahead = jnp.minimum(nt - 1 - me_t, NBACK) + 1
+    far = jnp.where(even, 2, 3)
+    ahead = 1 + jnp.where(me_t + 1 < nt, 1, 0) + jnp.where(me_t + far < nt, 1, 0)
     beside = jnp.minimum(me_r, NSIDE) + jnp.minimum(nr - 1 - me_r, NSIDE) + 1
     pl.semaphore_wait(barrier, ahead * beside - 1)
 
@@ -95,10 +106,24 @@
             device_id_type=pl.DeviceIdType.MESH,
         )
 
-    for n, (i, j) in reversed(list(enumerate(partners()))):
-        @pl.when(there(i, j))
-        def _():
-            copy(n, i, j).start()
+    def forward(n, i, j):
+        lo, hi = {2: (2, 5), -2: (0, 3)}.get(j, (0, 5))
+        return pltpu.make_async_remote_copy(
+            src_ref=R.at[NBACK - i, 2 - j, lo:hi],
+            dst_ref=R.at[NBACK - i - 1, 2 - j, lo:hi],
+            send_sem=fsem.at[n],
+            recv_sem=rsem.at[index[i + 1, j]],
+            device_id=to(1, 0),
+            device_id_type=pl.DeviceIdType.MESH,
+        )
+
+    index = {ij: n for n, ij in enumerate(partners())}
+    for i in ORDER:
+        for j in range(-NSIDE, NSIDE + 1):
+            if (i, j) in index:
+                @pl.when(sends(i, j))
+                def _():
+                    copy(index[i, j], i, j).start()
 
     WE[...] = jnp.zeros(WE.shape, BF)
     loads[1].wait()
@@ -136,14 +161,27 @@
 
     lax.fori_loop(0, 24, fold, 0)
 
+    relayed = [(i, j) for i in (1, 2) for j in range(-NSIDE, NSIDE + 1)]
+    for i, j in relayed:
+        @pl.when(there(-i, -j) & even)
+        def _():
+            copy(index[i, j], i, j).wait_recv()
+
+        @pl.when(there(-i, -j) & even & there(1, 0))
+        def _():
+            forward(index[i, j], i, j).start()
     for n, (i, j) in enumerate(partners()):
-        @pl.when(there(i, j))
+        @pl.when(there(-i, -j) & odd if (i, j) in relayed else there(-i, -j))
+        def _():
+            copy(n, i, j).wait_recv()
+    for n, (i, j) in enumerate(partners()):
+        @pl.when(sends(i, j))
         def _():
             copy(n, i, j).wait_send()
-
-        @pl.when(there(-i, -j))
-        def _():
-            copy(n, i, j).wait_recv()
+    for i, j in relayed:
+        @pl.when(there(-i, -j) & even & there(1, 0))
+        def _():
+            forward(index[i, j], i, j).wait_send()
 
 
 def exchange(nt, nr, lat, ek, uk, mk):
@@ -171,6 +209,7 @@
             pltpu.VMEM((3, 3, 3, C, C), BF),
             pltpu.VMEM((5, CI, 128), BF),
             pltpu.SemaphoreType.DMA((4,)),
+            pltpu.SemaphoreType.DMA((n,)),
             pltpu.SemaphoreType.DMA((n,)),
             pltpu.SemaphoreType.DMA((n,)),
         ],

time: 27.7 us -> 26.7 us (0.964)
  Pallas kernels: 27.6 us -> 26.5 us
    pallas_call x1, Pallas kernels: 15.3 us -> 14.2 us  [exchange(): pl.pallas_call(body, out_shape=(jax.ShapeDtypeStruct((4, 5, 5, CI, 128),...]
where the time goes in v6:
time: 26.7 us; the launch traced here: 26.5 us
  Pallas kernels  26.5 us (99%)
    pallas_call x1, Pallas kernels, exchange(): pl.pallas_call(body, out_shape=(jax.ShapeDtypeStruct((4, 5, 5, CI, 128),...  14.2 us
    pallas_call x1, Pallas kernels, decode(): pl.pallas_call(body, out_shape=jax.ShapeDtypeStruct((2, 4, 2 * W, C), BF)...  12.3 us

profile of v6, /device:TPU:1, one launch (start us, length us, event | category | flops | bytes accessed | tf_op | source)
XLA Modules:
  0.0 26.5 jit_solution(11763700657541726917)
XLA Ops:
  0.0 14.2 %exchange.1 = (bf16[4,5,5,16,128]{4,3,2,1,0:T(8,128)(2,1)S(1)}, bf16[3,256,1024]{2,1,0:T(8,128)(2,1)S(1)}, bf16[4,4,3,256,256]{4,3,2,1,0:T(8,128)(2,1)S(1)}, bf16[3,2,3,2,256,256]{5,4,3,2,1,0:T(8,128)(2,1)S(1)}) custom-call(bf16[2,2,16,160]{3,2,1,0:T(8,128)(2,1)} %bitcast.1, bf16[3,3,3,16,256]{4,3,2,1,0:T(8,128)(2,1)} %refs_1_.1, ...), custom_call_target="tpu_custom_call" | custom-call | tf_op jit(solution)/shard_map/exchange/pallas_call | solution.py:195
  14.2 12.3 %decode.1 = bf16[2,4,320,256]{3,2,1,0:T(8,128)(2,1)} custom-call(bf16[4,5,5,16,128]{4,3,2,1,0:T(8,128)(2,1)S(1)} %get-tuple-element.9.refs_0_, bf16[3,256,1024]{2,1,0:T(8,128)(2,1)S(1)} %get-tuple-element.10.refs_1_, bf16[4,4,3,256,256]{4,3,2,1,0:T(8,128)(2,1)S(1)} %get-tuple-element.11.refs_2_, bf16[3,2,3,2,256,256]{5,4,3,2,1,0:T(8,128)(2,1)S(1)} %get-tuple-element.12.refs_3_), custom_call_target="tpu_custom_call" | custom-call | tf_op jit(solution)/shard_map/decode/pallas_call | solution.py:346

commit v7 on v6

--- a/solution.py
+++ b/solution.py
@@ -12,7 +12,7 @@
 CI = 16
 NBACK = 3
 NSIDE = 2
-ORDER = (2, 1, 3, 0)
+ORDER = (2, 1, 0)
 
 
 def roll_cols(x, d):
@@ -63,10 +63,10 @@
     odd = lax.rem(me_t, 2) == 1
 
     def sends(i, j):
-        return there(i, j) & even if i == 2 else there(i, j) & odd if i == 3 else there(i, j)
+        return there(i, j) & even if i == 2 else there(i, j)
 
     def gets(i, j):
-        return there(-i, -j) & even if i >= 2 else there(-i, -j)
+        return there(-i, -j) & even if i == 2 else there(-i, -j)
 
     loads = [pltpu.make_async_copy(src, dst, lsem.at[n])
              for n, (src, dst) in enumerate(((lat_h, lat), (ek_h, ek), (uk, ubuf), (mk, mbuf)))]
@@ -74,9 +74,10 @@
         x.start()
     barrier = pltpu.get_barrier_semaphore()
     for i, j in partners():
-        @pl.when(gets(i, j))
-        def _():
-            pl.semaphore_signal(barrier, inc=1, device_id=to(-i, -j), device_id_type=pl.DeviceIdType.MESH)
+        if i < NBACK:
+            @pl.when(gets(i, j))
+            def _():
+                pl.semaphore_signal(barrier, inc=1, device_id=to(-i, -j), device_id_type=pl.DeviceIdType.MESH)
     for i, j in partners():
         @pl.when(jnp.logical_not(there(-i, -j)))
         def _():
@@ -90,8 +91,7 @@
             tails.append(v[:, 128:].astype(F32))
     pack[2] = jnp.concatenate(tails, axis=1).astype(BF)
     R[NBACK, 2] = pack[...]
-    far = jnp.where(even, 2, 3)
-    ahead = 1 + jnp.where(me_t + 1 < nt, 1, 0) + jnp.where(me_t + far < nt, 1, 0)
+    ahead = 1 + jnp.where(me_t + 1 < nt, 1, 0) + jnp.where(even & (me_t + 2 < nt), 1, 0)
     beside = jnp.minimum(me_r, NSIDE) + jnp.minimum(nr - 1 - me_r, NSIDE) + 1
     pl.semaphore_wait(barrier, ahead * beside - 1)
 
@@ -106,14 +106,14 @@
             device_id_type=pl.DeviceIdType.MESH,
         )
 
-    def forward(n, i, j):
+    def forward(i, j, step):
         lo, hi = {2: (2, 5), -2: (0, 3)}.get(j, (0, 5))
         return pltpu.make_async_remote_copy(
             src_ref=R.at[NBACK - i, 2 - j, lo:hi],
-            dst_ref=R.at[NBACK - i - 1, 2 - j, lo:hi],
-            send_sem=fsem.at[n],
-            recv_sem=rsem.at[index[i + 1, j]],
-            device_id=to(1, 0),
+            dst_ref=R.at[NBACK - i - step, 2 - j, lo:hi],
+            send_sem=fsem.at[step - 1, index[i, j]],
+            recv_sem=rsem.at[index[i + step, j]],
+            device_id=to(step, 0),
             device_id_type=pl.DeviceIdType.MESH,
         )
 
@@ -167,21 +167,24 @@
         def _():
             copy(index[i, j], i, j).wait_recv()
 
-        @pl.when(there(-i, -j) & even & there(1, 0))
-        def _():
-            forward(index[i, j], i, j).start()
+        for step in (2, 1)[i - 1:]:
+            @pl.when(there(-i, -j) & even & there(step, 0))
+            def _():
+                forward(i, j, step).start()
     for n, (i, j) in enumerate(partners()):
         @pl.when(there(-i, -j) & odd if (i, j) in relayed else there(-i, -j))
         def _():
             copy(n, i, j).wait_recv()
     for n, (i, j) in enumerate(partners()):
-        @pl.when(sends(i, j))
-        def _():
-            copy(n, i, j).wait_send()
+        if i < NBACK:
+            @pl.when(sends(i, j))
+            def _():
+                copy(n, i, j).wait_send()
     for i, j in relayed:
-        @pl.when(there(-i, -j) & even & there(1, 0))
-        def _():
-            forward(index[i, j], i, j).wait_send()
+        for step in (2, 1)[i - 1:]:
+            @pl.when(there(-i, -j) & even & there(step, 0))
+            def _():
+                forward(i, j, step).wait_send()
 
 
 def exchange(nt, nr, lat, ek, uk, mk):
@@ -211,7 +214,7 @@
             pltpu.SemaphoreType.DMA((4,)),
             pltpu.SemaphoreType.DMA((n,)),
             pltpu.SemaphoreType.DMA((n,)),
-            pltpu.SemaphoreType.DMA((n,)),
+            pltpu.SemaphoreType.DMA((2, n)),
         ],
         compiler_params=pltpu.CompilerParams(collective_id=0, has_side_effects=True, vmem_limit_bytes=16 * 2**20),
         name="exchange",
@@ -303,12 +306,12 @@
             else:
                 finish(1, h, Y[1, h] - z)
 
-    def prod(a, b):
+    def prod(a, b, frames=(0, 1)):
         acc = None
         for dt in (2, 1, 0):
             for c in range(2):
                 parts = []
-                for t in range(2):
+                for t in frames:
                     for q in range(2):
                         x = [S3[b + c, t + dt, q + k] for k in ((0, 1), (1,), (1, 2))[a]]
                         parts.append(x[0] if a == 1 else x[0] - x[1] if a == 0 else x[1] - x[0])
@@ -322,13 +325,16 @@
 
     for b in range(2):
         CR[b] = prod(1, b)
-    for a in range(2):
+    for a, frames in ((0, (0, 1)), (1, (0,)), (1, (1,))):
+        cells = [2 * t + q for t in frames for q in range(2)]
+        lo = cells[0] * W
+        hi = lo + len(cells) * W
         for b in range(2):
-            y = silu(prod(2 * a, b) + CR[b])
-            for i in range(4):
+            y = silu(prod(2 * a, b, frames) + CR[b, lo:hi])
+            for i in cells:
                 for h in range(2):
-                    I[i, h, pl.ds(b, W, stride=2), :] = y[i * W:(i + 1) * W, h * 128:(h + 1) * 128]
-        for i in range(4):
+                    I[i, h, pl.ds(b, W, stride=2), :] = y[i * W - lo:(i + 1) * W - lo, h * 128:(h + 1) * 128]
+        for i in cells:
             for h in range(2):
                 out[i // 2, 2 * (i % 2) + a, :, h * 128:(h + 1) * 128] = I[i, h].astype(BF)
             store(a, i).start()

time: 26.7 us -> 26.3 us (0.985)
  the two profiles are of different devices: /device:TPU:1 before, /device:TPU:22 now
where the time goes in v7:
time: 26.3 us
  Pallas kernels  26.2 us (100%)
    pallas_call x1, Pallas kernels, exchange(): pl.pallas_call(body, out_shape=(jax.ShapeDtypeStruct((4, 5, 5, CI, 128),...  14 us
    pallas_call x1, Pallas kernels, decode(): pl.pallas_call(body, out_shape=jax.ShapeDtypeStruct((2, 4, 2 * W, C), BF)...  12.3 us

profile of v7, /device:TPU:22, one launch (start us, length us, event | category | flops | bytes accessed | tf_op | source)
XLA Modules:
  0.0 26.3 jit_solution(14561978392870656188)
XLA Ops:
  0.0 14.0 %exchange.1 = (bf16[4,5,5,16,128]{4,3,2,1,0:T(8,128)(2,1)S(1)}, bf16[3,256,1024]{2,1,0:T(8,128)(2,1)S(1)}, bf16[4,4,3,256,256]{4,3,2,1,0:T(8,128)(2,1)S(1)}, bf16[3,2,3,2,256,256]{5,4,3,2,1,0:T(8,128)(2,1)S(1)}) custom-call(bf16[2,2,16,160]{3,2,1,0:T(8,128)(2,1)} %bitcast.1, bf16[3,3,3,16,256]{4,3,2,1,0:T(8,128)(2,1)} %refs_1_.1, ...), custom_call_target="tpu_custom_call" | custom-call | tf_op jit(solution)/shard_map/exchange/pallas_call | solution.py:198
  14.0 12.3 %decode.1 = bf16[2,4,320,256]{3,2,1,0:T(8,128)(2,1)} custom-call(bf16[4,5,5,16,128]{4,3,2,1,0:T(8,128)(2,1)S(1)} %get-tuple-element.9.refs_0_, bf16[3,256,1024]{2,1,0:T(8,128)(2,1)S(1)} %get-tuple-element.10.refs_1_, bf16[4,4,3,256,256]{4,3,2,1,0:T(8,128)(2,1)S(1)} %get-tuple-element.11.refs_2_, bf16[3,2,3,2,256,256]{5,4,3,2,1,0:T(8,128)(2,1)S(1)} %get-tuple-element.12.refs_3_), custom_call_target="tpu_custom_call" | custom-call | tf_op jit(solution)/shard_map/decode/pallas_call | solution.py:352
